TPU v7x, 32 devices: a whole 2x2x4 slice. The times are simulated.
32 devices in a mesh: dp: 4 (over x, y), tp: 8 (over z, core).
Axes of the slice: x: 2, y: 2, z: 4, core: 2. Of those that a mesh axis runs over, the one named last changes fastest.
Arguments:
- X: bfloat16 [1024, 2048], P(('dp', 'tp')), parts along dimension 0
- dY: bfloat16 [1024, 2048], P(('dp', 'tp')), parts along dimension 0
- W1: bfloat16 [2048, 8192], P(None, 'tp')
- W2: bfloat16 [8192, 2048], P('tp')
Outputs:
- output 1: bfloat16 [1024, 2048], P(('dp', 'tp')), parts along dimension 0
- output 2: float32 [8192, 8192], P('dp', 'tp'), parts along dimension 0
- output 3: float32 [32768, 2048], P(('dp', 'tp')), parts along dimension 0
There are 4 independent parts. A program takes and returns all parts, laid end to end along the dimension named above; an argument that names none is the same for every part.
All inputs are finite; a program needn't handle non-finite values.
Results may differ from a plain program's by a relative error of at most 0.00939837.
Values are sent between devices in bfloat16 or wider.
A program may use at most 1 GiB of HBM per device.

v0:
```python
import math
import jax
import jax.numpy as jnp
from jax import lax
from jax.sharding import PartitionSpec as P

C0 = math.sqrt(2.0 / math.pi)
C1 = 0.044715


def _gelu(u):
    t = jnp.tanh(C0 * (u + C1 * u * u * u))
    return 0.5 * u * (1.0 + t), 0.5 * (1.0 + t) + 0.5 * u * (1.0 - t * t) * C0 * (1.0 + 3.0 * C1 * u * u)


def solution(mesh):
    def body(x, dy, w1, w2):
        xg = lax.all_gather(x, 'tp', axis=0, tiled=True)
        dyg = lax.all_gather(dy, 'tp', axis=0, tiled=True)
        u = jnp.dot(xg, w1, preferred_element_type=jnp.float32).astype(jnp.bfloat16)
        g0, g1 = _gelu(u.astype(jnp.float32))
        z = g0.astype(jnp.bfloat16)
        dw2 = jnp.dot(z.T, dyg, preferred_element_type=jnp.float32)
        g = jnp.dot(dyg, w2.T, preferred_element_type=jnp.float32)
        dz = (g * g1).astype(jnp.bfloat16)
        pdx = jnp.dot(dz, w1.T, preferred_element_type=jnp.float32)
        dx = lax.psum_scatter(pdx, 'tp', scatter_dimension=0, tiled=True).astype(jnp.bfloat16)
        dw1 = jnp.dot(xg.T, dz, preferred_element_type=jnp.float32)
        return dx, dw1, dw2

    return jax.shard_map(
        body, mesh=mesh,
        in_specs=(P(('dp', 'tp'), None), P(('dp', 'tp'), None), P(None, 'tp'), P('tp', None)),
        out_specs=(P(('dp', 'tp'), None), P('dp', 'tp'), P(('dp', 'tp'), None)),
        check_vma=False)
```

profile of v0, /device:TPU:0, one launch (start us, length us, event | category | flops | bytes accessed | tf_op | source)
XLA Modules:
  0.0 109.3 jit_solution(13943951119200912984)
XLA Ops:
  7.2 0.0 all-gather.5.cloned.1.call-start
  7.2 0.7 all-gather.5.cloned.1.call-update
  7.9 0.0 all-gather.3.cloned.1.call-start
  7.9 0.7 all-gather.3.cloned.1.call-update
  8.6 0.0 reduce-scatter.2.cloned.1.call-start
  8.7 26.1 %all-gather.5.cloned.1.call-done = bf16[256,2048]{1,0:T(8,128)(2,1)} async-done(((bf16[32,2048]{1,0:T(8,128)(2,1)}), bf16[256,2048]{1,0:T(8,128)(2,1)}) %all-gather.5.cloned.1.call-update) | async-done | bytes 1048592 | tf_op jit(solution)/shard_map/all_gather | solution.py:18
  34.8 3.8 %convolution_convert_fusion = bf16[256,1024]{1,0:T(8,128)(2,1)S(1)} fusion(bf16[256,2048]{1,0:T(8,128)(2,1)} %all-gather.5.cloned.1.call-done, bf16[2048,1024]{1,0:T(8,128)(2,1)} %param.6), kind=kOutput, calls=%fused_computation.10 | convolution fusion | flops 1074003968 | bytes 5767168 | tf_op jit(solution)/shard_map/dot_general | solution.py:20
  38.6 19.9 %all-gather.3.cloned.1.call-done = bf16[256,2048]{1,0:T(8,128)(2,1)} async-done(((bf16[32,2048]{1,0:T(8,128)(2,1)}), bf16[256,2048]{1,0:T(8,128)(2,1)}) %all-gather.3.cloned.1.call-update) | async-done | bytes 1048592 | tf_op jit(solution)/shard_map/all_gather | solution.py:19
  58.5 0.0 copy-start.2
  58.5 4.4 %fusion = bf16[256,1024]{1,0:T(8,128)(2,1)S(1)} fusion(bf16[256,2048]{1,0:T(8,128)(2,1)} %all-gather.3.cloned.1.call-done, bf16[1024,2048]{1,0:T(8,128)(2,1)} %param.7, bf16[256,1024]{1,0:T(8,128)(2,1)S(1)} %convolution_convert_fusion), kind=kOutput, calls=%fused_computation.9 | convolution fusion | flops 1078984704 | bytes 6291456 | tf_op jit(solution)/shard_map/dot_general | solution.py:24
  62.9 0.0 copy-done.2
  62.9 0.0 copy-start
  63.0 2.6 %fusion.20 = f32[256,2048]{1,0:T(8,128)} fusion(bf16[256,1024]{1,0:T(8,128)(2,1)S(1)} %fusion, bf16[2048,1024]{1,0:T(8,128)(2,1)S(1)} %copy-done.2), kind=kOutput, calls=%fused_computation.29 | convolution fusion | flops 1073741824 | bytes 6815744 | tf_op jit(solution)/shard_map/dot_general | solution.py:26
  65.6 0.0 reduce-scatter.2.cloned.1.call-update
  65.6 0.0 copy-done
  65.6 4.7 %convolution_bitcast_fusion = f32[2048,1024]{0,1:T(8,128)} fusion(bf16[256,1024]{1,0:T(8,128)(2,1)S(1)} %fusion, bf16[256,2048]{1,0:T(8,128)(2,1)S(1)} %copy-done), kind=kOutput, calls=%fused_computation | convolution fusion | flops 1073741824 | bytes 9961472 | tf_op jit(solution)/shard_map/dot_general | solution.py:28
  70.3 0.0 copy-start.1
  70.3 9.3 %copy.7 = f32[2048,1024]{1,0:T(8,128)} copy(f32[2048,1024]{0,1:T(8,128)} %convolution_bitcast_fusion) | data formatting | bytes 16777216
  79.6 0.0 copy-done.1
  79.6 4.9 %fusion.10 = f32[1024,2048]{1,0:T(8,128)} fusion(bf16[256,2048]{1,0:T(8,128)(2,1)S(1)} %copy-done.1, bf16[256,1024]{1,0:T(8,128)(2,1)S(1)} %convolution_convert_fusion), kind=kOutput, calls=%fused_computation.20 | convolution fusion | flops 1076363264 | bytes 9961472 | tf_op jit(solution)/shard_map/dot_general | solution.py:23
  84.6 16.6 %reduce-scatter.2.cloned.1.call-done = f32[32,2048]{1,0:T(8,128)} async-done(((f32[256,2048]{1,0:T(8,128)}), f32[32,2048]{1,0:T(8,128)}) %reduce-scatter.2.cloned.1.call-update) | async-done | bytes 262160 | tf_op jit(solution)/shard_map/reduce_scatter | solution.py:27
  101.2 1.6 %convert_element_type.18 = bf16[32,2048]{1,0:T(8,128)(2,1)} convert(f32[32,2048]{1,0:T(8,128)} %reduce-scatter.2.cloned.1.call-done) | non-fusion elementwise | flops 65536 | bytes 393216 | tf_op jit(solution)/shard_map/convert_element_type | solution.py:27
Async XLA Ops:
  7.2 27.6 %all-gather.5.cloned.1.call-start = ((), (), s32[]{:S(2)}) async-start(), calls=%async_computation.2 | async-start | bytes 1179648 | tf_op jit(solution)/shard_map/all_gather | solution.py:18
  7.9 50.6 %all-gather.3.cloned.1.call-start = ((), (), s32[]{:S(2)}) async-start(), calls=%async_computation.1 | async-start | bytes 1179648 | tf_op jit(solution)/shard_map/all_gather | solution.py:19
  8.6 92.5 %reduce-scatter.2.cloned.1.call-start = ((), (), s32[]{:S(2)}) async-start(), calls=%async_computation.3 | async-start | bytes 2359296 | tf_op jit(solution)/shard_map/reduce_scatter | solution.py:27
  58.5 4.4 %copy-start.2 = (bf16[2048,1024]{1,0:T(8,128)(2,1)S(1)}, bf16[2048,1024]{1,0:T(8,128)(2,1)}, u32[]{:S(2)}) copy-start(bf16[2048,1024]{1,0:T(8,128)(2,1)} %param.6) | copy-start | bytes 12582916
  62.9 2.7 %copy-start = (bf16[256,2048]{1,0:T(8,128)(2,1)S(1)}, bf16[256,2048]{1,0:T(8,128)(2,1)}, u32[]{:S(2)}) copy-start(bf16[256,2048]{1,0:T(8,128)(2,1)} %all-gather.5.cloned.1.call-done) | copy-start | bytes 3145732
  70.3 9.3 %copy-start.1 = (bf16[256,2048]{1,0:T(8,128)(2,1)S(1)}, bf16[256,2048]{1,0:T(8,128)(2,1)}, u32[]{:S(2)}) copy-start(bf16[256,2048]{1,0:T(8,128)(2,1)} %all-gather.3.cloned.1.call-done) | copy-start | bytes 3145732
Sparse Core Ops, SparseCore 0:
  9.6 25.1 all-gather.4
  36.4 22.0 all-gather.2
  65.7 35.4 reduce-scatter.1
where the time goes:
time: 110 us; the launch traced here: 109 us
  waiting for transfers between devices  64.1 us (58%)
  matrix products  20.4 us (19%)
  between operations  13.8 us (13%)
  local copies, waits for them, and re-layouts  9.34 us (8%)
  other arithmetic  1.62 us (1%)
    all_gather x1, waiting for transfers between devices, body(): xg = lax.all_gather(x, 'tp', axis=0, tiled=True)  26.1 us
    all_gather x1, waiting for transfers between devices, body(): dyg = lax.all_gather(dy, 'tp', axis=0, tiled=True)  19.9 us
    reduce_scatter x1, waiting for transfers between devices, body(): lax.psum_scatter(pdx, 'tp', scatter_dimension=0, tiled=True)  16.6 us
    unnamed x7, local copies, waits for them, and re-layouts  9.34 us
    dot_general x1, matrix products, body(): dw2 = jnp.dot(z.T, dyg, preferred_element_type=jnp.float32)  4.92 us
    dot_general x1, matrix products, body(): dw1 = jnp.dot(xg.T, dz, preferred_element_type=jnp.float32)  4.69 us
    dot_general x1, matrix products, body(): g = jnp.dot(dyg, w2.T, preferred_element_type=jnp.float32)  4.42 us
    dot_general x1, matrix products, body(): u = jnp.dot(xg, w1, preferred_element_type=jnp.float32).astype(jnp.bfloat16)  3.76 us
  transfers between devices with their start and end apart: 3, of which 3 were waited for; matrix products, arithmetic and copies ran while one was open for 21% of the time, Pallas kernels for 0%

commit v1 on v0

v1 whole, which is shorter than its diff:
```python
import math

import jax
import jax.numpy as jnp
from jax import lax
from jax.experimental import pallas as pl
from jax.experimental.pallas import tpu as pltpu
from jax.sharding import PartitionSpec as P

C0 = math.sqrt(2.0 / math.pi)
C1 = 0.044715
BF16 = jnp.bfloat16
F32 = jnp.float32
X, Y = 0, 1
LEFT, RIGHT, PARTNER = 0, 1, 2
MIB = 1 << 20


def _gelu(u):
    t = jnp.tanh(C0 * (u + C1 * u * u * u))
    return 0.5 * u * (1.0 + t), 0.5 * (1.0 + t) + 0.5 * u * (1.0 - t * t) * C0 * (1.0 + 3.0 * C1 * u * u)


def _slot_of(z, q):
    qm = jnp.where(z < 2, q, 3 - q)
    end = jnp.logical_or(z == 0, z == 3)
    return jnp.where(jnp.logical_or(end, qm == 3), qm, (qm + 2) % 3)


def _chip_at(z, k):
    end = jnp.logical_or(z == 0, z == 3)
    qm = k if k == 3 else jnp.where(end, k, (k + 1) % 3)
    return jnp.where(z < 2, qm, 3 - qm)


def _gather_kernel(rows, x_hbm, y_hbm, w1_hbm, w2_hbm,
                   xo, yo, zo, dzo, dx_ref,
                   xg, yg, zs, dzs, g1s, w1, w2, w1t, w2t, pdx, psend, precv, rsend, rrecv,
                   in_sem, w_sem, out_sem, ag_send, ag_recv, ag_precv,
                   p_send, p_recv, r_send, r_recv):
    t = lax.axis_index('tp')
    z, c = t // 2, t % 2
    chunk = 2 * rows
    f, h = w2.shape
    has_left, has_right = z > 0, z < 3
    bufs = (xg, yg)

    def dev(chip, core):
        return {'tp': 2 * chip + core}

    def block(a, slot, core):
        return bufs[a].at[pl.ds(pl.multiple_of(slot * chunk + core * rows, rows), rows), :]

    loads = [pltpu.make_async_copy(src, block(a, 0, c), in_sem.at[a]) for a, src in ((X, x_hbm), (Y, y_hbm))]
    wloads = [pltpu.make_async_copy(src, dst, w_sem.at[i]) for i, (src, dst) in enumerate(((w2_hbm, w2), (w1_hbm, w1)))]
    for cp in loads + wloads:
        cp.start()

    barrier = pltpu.get_barrier_semaphore()
    pl.semaphore_signal(barrier, inc=1, device_id=dev(z, 1 - c), device_id_type=pl.DeviceIdType.MESH)

    @pl.when(has_left)
    def _():
        pl.semaphore_signal(barrier, inc=1, device_id=dev(z - 1, c), device_id_type=pl.DeviceIdType.MESH)

    @pl.when(has_right)
    def _():
        pl.semaphore_signal(barrier, inc=1, device_id=dev(z + 1, c), device_id_type=pl.DeviceIdType.MESH)

    @pl.when(jnp.logical_and(has_left, has_right))
    def _():
        pl.semaphore_wait(barrier, 3)

    @pl.when(jnp.logical_not(jnp.logical_and(has_left, has_right)))
    def _():
        pl.semaphore_wait(barrier, 2)

    def ag_copy(a, q, to):
        chip = {LEFT: z - 1, RIGHT: z + 1, PARTNER: z}[to]
        core = 1 - c if to == PARTNER else c
        recv = ag_precv if to == PARTNER else ag_recv
        return pltpu.make_async_remote_copy(
            src_ref=block(a, _slot_of(z, q), c), dst_ref=block(a, _slot_of(chip, q), c),
            send_sem=ag_send.at[to, a, q], recv_sem=recv.at[a, q],
            device_id=dev(chip, core), device_id_type=pl.DeviceIdType.MESH)

    def ag_forward(a, q, to):
        ok = {LEFT: has_left, RIGHT: has_right}[to]

        @pl.when(ok)
        def _():
            ag_copy(a, q, to).start()

    def ag_wait(a, q, core, recv):
        dst = block(a, _slot_of(z, q), core)
        pltpu.make_async_copy(dst, dst, recv.at[a, q]).wait()

    for a in (X, Y):
        loads[a].wait()
        ag_forward(a, z, RIGHT)
        ag_forward(a, z, LEFT)
        ag_copy(a, z, PARTNER).start()

    def arrivals(a, d):
        @pl.when(z - d >= 0)
        def _():
            ag_wait(a, z - d, c, ag_recv)
            ag_forward(a, z - d, RIGHT)
            ag_copy(a, z - d, PARTNER).start()

        @pl.when(z + d <= 3)
        def _():
            ag_wait(a, z + d, c, ag_recv)
            ag_forward(a, z + d, LEFT)
            ag_copy(a, z + d, PARTNER).start()

    def partner_wait(a, k):
        ag_wait(a, _chip_at(z, k), 1 - c, ag_precv)

    wloads[0].wait()

    @pl.loop(0, f // 256)
    def _(i):
        s = pl.ds(pl.multiple_of(i * 256, 256), 256)
        w2t[:, s] = w2[s, :].T

    wloads[1].wait()

    @pl.loop(0, h // 256)
    def _(i):
        s = pl.ds(pl.multiple_of(i * 256, 256), 256)
        w1t[:, s] = w1[s, :].T

    def step_u(r0, m):
        r = pl.ds(r0, m)

        @pl.loop(0, f // 512)
        def _(n):
            s = pl.ds(pl.multiple_of(n * 512, 512), 512)
            u = jnp.dot(xg[r, :], w1[:, s], preferred_element_type=F32).astype(BF16)
            g0, g1 = _gelu(u.astype(F32))
            zs[r, s] = g0.astype(BF16)
            g1s[r, s] = g1

    def step_g(r0, m):
        r = pl.ds(r0, m)

        @pl.loop(0, f // 512)
        def _(n):
            s = pl.ds(pl.multiple_of(n * 512, 512), 512)
            g = jnp.dot(yg[r, :], w2t[:, s], preferred_element_type=F32)
            dzs[r, s] = (g * g1s[r, s]).astype(BF16)

    def step_dx(r0, m):
        r = pl.ds(r0, m)

        @pl.loop(0, h // 512)
        def _(n):
            s = pl.ds(pl.multiple_of(n * 512, 512), 512)
            pdx[r, s] = jnp.dot(dzs[r, :], w1t[:, s], preferred_element_type=F32)

    def pair_copy(k):
        return pltpu.make_async_remote_copy(
            src_ref=psend.at[k], dst_ref=precv.at[k], send_sem=p_send.at[k], recv_sem=p_recv.at[k],
            device_id=dev(z, 1 - c), device_id_type=pl.DeviceIdType.MESH)

    def rs_copy(k):
        q = _chip_at(z, k)
        s = _slot_of(q, z)
        return pltpu.make_async_remote_copy(
            src_ref=rsend.at[k], dst_ref=rrecv.at[s], send_sem=r_send.at[k], recv_sem=r_recv.at[s],
            device_id=dev(q, c), device_id_type=pl.DeviceIdType.MESH)

    def part(k, core):
        return pdx[pl.ds(pl.multiple_of(k * chunk + core * rows, rows), rows), :]

    def pair_start(k):
        psend[k] = part(k, 1 - c).astype(BF16)
        pair_copy(k).start()

    def rs_start(k):
        pair_copy(k).wait_recv()
        rsend[k] = (part(k, c) + precv[k].astype(F32)).astype(BF16)
        rs_copy(k).start()

    arrivals(X, 1)
    partner_wait(X, 0)
    step_u(0, chunk)
    partner_wait(Y, 0)
    step_g(0, chunk)
    arrivals(Y, 1)
    step_dx(0, chunk)
    pair_start(0)
    arrivals(X, 2)
    partner_wait(X, 1)
    partner_wait(X, 2)
    step_u(chunk, 2 * chunk)
    arrivals(Y, 2)
    partner_wait(Y, 1)
    partner_wait(Y, 2)
    step_g(chunk, 2 * chunk)
    step_dx(chunk, 2 * chunk)
    pair_start(1)
    pair_start(2)
    rs_start(1)
    rs_start(2)
    arrivals(X, 3)
    partner_wait(X, 3)
    xout = pltpu.make_async_copy(xg, xo, out_sem.at[0])
    xout.start()
    step_u(3 * chunk, chunk)
    zout = pltpu.make_async_copy(zs, zo, out_sem.at[1])
    zout.start()
    arrivals(Y, 3)
    partner_wait(Y, 3)
    yout = pltpu.make_async_copy(yg, yo, out_sem.at[2])
    yout.start()
    step_g(3 * chunk, chunk)
    dzout = pltpu.make_async_copy(dzs, dzo, out_sem.at[3])
    dzout.start()
    step_dx(3 * chunk, chunk)
    pair_start(3)
    rs_start(3)

    pair_copy(0).wait_recv()
    total = part(0, c) + precv[0].astype(F32)
    for k in (1, 2, 3):
        pltpu.make_async_copy(rrecv.at[k], rrecv.at[k], r_recv.at[k]).wait()
        total += rrecv[k].astype(F32)
    dx_ref[...] = total.astype(BF16)

    def ag_drain(a, q, to):
        ok = {LEFT: has_left, RIGHT: has_right}[to]

        @pl.when(ok)
        def _():
            ag_copy(a, q, to).wait_send()

    for a in (X, Y):
        ag_drain(a, z, RIGHT)
        ag_drain(a, z, LEFT)
        ag_copy(a, z, PARTNER).wait_send()
        for d in (1, 2, 3):
            @pl.when(z - d >= 0)
            def _():
                ag_drain(a, z - d, RIGHT)
                ag_copy(a, z - d, PARTNER).wait_send()

            @pl.when(z + d <= 3)
            def _():
                ag_drain(a, z + d, LEFT)
                ag_copy(a, z + d, PARTNER).wait_send()
    for k in range(4):
        pair_copy(k).wait_send()
    for k in (1, 2, 3):
        rs_copy(k).wait_send()
    for cp in (xout, yout, zout, dzout):
        cp.wait()


def _dw_kernel(xb, dz, zb, y, dxi, dw1, dw2, dx):
    dims = (((0,), (0,)), ((), ()))
    dw1[...] = lax.dot_general(xb[...], dz[...], dims, preferred_element_type=F32)
    dw2[...] = lax.dot_general(zb[...], y[...], dims, preferred_element_type=F32)

    @pl.when(pl.program_id(0) == 0)
    def _():
        dx[...] = dxi[...]


def solution(mesh):
    def body(x, dy, w1, w2):
        rows, h = x.shape
        f = w1.shape[1]
        n = 8 * rows
        vm = pltpu.VMEM
        sem = pltpu.SemaphoreType.DMA
        anyspec = pl.BlockSpec(memory_space=pl.ANY)
        xg, yg, zg, dzg, dx = pl.pallas_call(
            lambda *refs: _gather_kernel(rows, *refs),
            out_shape=(
                jax.ShapeDtypeStruct((n, h), BF16), jax.ShapeDtypeStruct((n, h), BF16),
                jax.ShapeDtypeStruct((n, f), BF16), jax.ShapeDtypeStruct((n, f), BF16),
                jax.ShapeDtypeStruct((rows, h), BF16)),
            in_specs=[anyspec] * 4,
            out_specs=(anyspec,) * 4 + (pl.BlockSpec(memory_space=pltpu.VMEM),),
            scratch_shapes=[
                vm((n, h), BF16), vm((n, h), BF16), vm((n, f), BF16), vm((n, f), BF16), vm((n, f), F32),
                vm((h, f), BF16), vm((f, h), BF16), vm((f, h), BF16), vm((h, f), BF16),
                vm((n, h), F32), vm((4, rows, h), BF16), vm((4, rows, h), BF16),
                vm((4, rows, h), BF16), vm((4, rows, h), BF16),
                sem((2,)), sem((2,)), sem((4,)), sem((3, 2, 4)), sem((2, 4)), sem((2, 4)),
                sem((4,)), sem((4,)), sem((4,)), sem((4,)),
            ],
            compiler_params=pltpu.CompilerParams(
                collective_id=0, has_side_effects=True, vmem_limit_bytes=56 * MIB),
            name='gather_dx',
        )(x, dy, w1, w2)
        steps = 8
        hb, fb = h // steps, f // steps
        dw1, dw2, dx = pl.pallas_call(
            _dw_kernel,
            grid=(steps,),
            out_shape=(jax.ShapeDtypeStruct((h, f), F32), jax.ShapeDtypeStruct((f, h), F32),
                       jax.ShapeDtypeStruct((rows, h), BF16)),
            in_specs=[
                pl.BlockSpec((n, hb), lambda i: (0, i)), pl.BlockSpec((n, f), lambda i: (0, 0)),
                pl.BlockSpec((n, fb), lambda i: (0, i)), pl.BlockSpec((n, h), lambda i: (0, 0)),
                pl.BlockSpec((rows, h), lambda i: (0, 0)),
            ],
            out_specs=(
                pl.BlockSpec((hb, f), lambda i: (i, 0)), pl.BlockSpec((fb, h), lambda i: (i, 0)),
                pl.BlockSpec((rows, h), lambda i: (0, 0)),
            ),
            compiler_params=pltpu.CompilerParams(vmem_limit_bytes=40 * MIB),
            name='dw',
        )(xg, dzg, zg, yg, dx)
        return dx, dw1, dw2

    return jax.shard_map(
        body, mesh=mesh,
        in_specs=(P(('dp', 'tp'), None), P(('dp', 'tp'), None), P(None, 'tp'), P('tp', None)),
        out_specs=(P(('dp', 'tp'), None), P('dp', 'tp'), P(('dp', 'tp'), None)),
        check_vma=False)
```

time: 110 us -> 52.4 us (0.48)
  waiting for transfers between devices: 64.1 us -> 0 us
  Pallas kernels: 0 us -> 46 us
  matrix products: 20.4 us -> 0 us
  between operations: 13.8 us -> 0.65 us
  local copies, waits for them, and re-layouts: 9.34 us -> 5.43 us
  other arithmetic: 1.62 us -> 0 us
    all_gather x2 -> x0, waiting for transfers between devices: 46 us -> none  [the longest x1 26.1 us: body(): xg = lax.all_gather(x, 'tp', axis=0, tiled=True)]
    pallas_call x0 -> x2, Pallas kernels: none -> 46 us  [the longest x1 38.2 us: body(): pl.pallas_call(lambda *refs: _gather_kernel(rows, *refs), out_shape=(jax....]
    dot_general x5 -> x0, matrix products: 20.4 us -> none  [the longest x1 4.92 us: body(): dw2 = jnp.dot(z.T, dyg, preferred_element_type=jnp.float32)]
    reduce_scatter x1 -> x0, waiting for transfers between devices: 16.6 us -> none  [body(): lax.psum_scatter(pdx, 'tp', scatter_dimension=0, tiled=True)]
    unnamed x7 -> x10, local copies, waits for them, and re-layouts: 9.34 us -> 5.43 us
    convert_element_type x1 -> x0, other arithmetic: 1.62 us -> none  [body(): lax.psum_scatter(pdx, 'tp', scatter_dimension=0, tiled=True)]
    unnamed x3 -> x0, waiting for transfers between devices: 1.39 us -> none
  transfers between devices with their start and end apart: 3 -> 0, of which waited for: 3 -> 0; matrix products, arithmetic and copies ran while one was open for 21% -> 0% of each run, Pallas kernels for 0% -> 0%
where the time goes in v1:
time: 52.4 us; the launch traced here: 52.1 us
  Pallas kernels  46 us (88%)
  local copies, waits for them, and re-layouts  5.43 us (10%)
  between operations  0.65 us (1%)
    pallas_call x1, Pallas kernels, body(): pl.pallas_call(lambda *refs: _gather_kernel(rows, *refs), out_shape=(jax....  38.2 us
    pallas_call x1, Pallas kernels, body(): pl.pallas_call(_dw_kernel, grid=(steps,), out_shape=(jax.ShapeDtypeStruct...  7.88 us
    unnamed x10, local copies, waits for them, and re-layouts  5.43 us

profile of v1, /device:TPU:0, one launch (start us, length us, event | category | flops | bytes accessed | tf_op | source)
XLA Modules:
  0.0 52.1 jit_solution(11554375663498234301)
XLA Ops:
  0.6 38.2 %gather_dx.1 = (bf16[256,2048]{1,0:T(8,128)(2,1)}, bf16[256,2048]{1,0:T(8,128)(2,1)}, bf16[256,1024]{1,0:T(8,128)(2,1)}, bf16[256,1024]{1,0:T(8,128)(2,1)}, bf16[32,2048]{1,0:T(8,128)(2,1)}) custom-call(bf16[32,2048]{1,0:T(8,128)(2,1)} %refs_0_.1, bf16[32,2048]{1,0:T(8,128)(2,1)} %refs_1_.1, bf16[2048,1024]{1,0:T(8,128)(2,1)} %refs_2_.1, ...), custom_call_target="tpu_custom_call" | custom-call | tf_op jit(solution)/shard_map/gather_dx/pallas_call | solution.py:279
  38.8 0.0 copy-start
  38.8 1.2 %copy-done = bf16[256,2048]{1,0:T(8,128)(2,1)S(1)} copy-done((bf16[256,2048]{1,0:T(8,128)(2,1)S(1)}, bf16[256,2048]{1,0:T(8,128)(2,1)}, u32[]{:S(2)}) %copy-start) | copy-done | bytes 1048600
  40.0 0.0 copy-start.1
  40.0 1.2 %copy-done.1 = bf16[256,2048]{1,0:T(8,128)(2,1)S(1)} copy-done((bf16[256,2048]{1,0:T(8,128)(2,1)S(1)}, bf16[256,2048]{1,0:T(8,128)(2,1)}, u32[]{:S(2)}) %copy-start.1) | copy-done | bytes 1048600
  41.2 0.0 copy-start.2
  41.2 1.0 %copy-done.2 = bf16[256,1024]{1,0:T(8,128)(2,1)S(1)} copy-done((bf16[256,1024]{1,0:T(8,128)(2,1)S(1)}, bf16[256,1024]{1,0:T(8,128)(2,1)}, u32[]{:S(2)}) %copy-start.2) | copy-done | bytes 524312
  42.3 0.0 copy-start.3
  42.3 1.0 %copy-done.3 = bf16[256,1024]{1,0:T(8,128)(2,1)S(1)} copy-done((bf16[256,1024]{1,0:T(8,128)(2,1)S(1)}, bf16[256,1024]{1,0:T(8,128)(2,1)}, u32[]{:S(2)}) %copy-start.3) | copy-done | bytes 524312
  43.3 0.0 copy-start.4
  43.3 0.9 %copy-done.4 = bf16[32,2048]{1,0:T(8,128)(2,1)S(1)} copy-done((bf16[32,2048]{1,0:T(8,128)(2,1)S(1)}, bf16[32,2048]{1,0:T(8,128)(2,1)}, u32[]{:S(2)}) %copy-start.4) | copy-done | bytes 131096
  44.2 7.9 %dw.1 = (f32[2048,1024]{1,0:T(8,128)}, f32[1024,2048]{1,0:T(8,128)}, bf16[32,2048]{1,0:T(8,128)(2,1)}) custom-call(bf16[256,2048]{1,0:T(8,128)(2,1)S(1)} %copy-done, bf16[256,1024]{1,0:T(8,128)(2,1)S(1)} %copy-done.3, bf16[256,1024]{1,0:T(8,128)(2,1)S(1)} %copy-done.2, bf16[256,2048]{1,0:T(8,128)(2,1)S(1)} %copy-done.1, bf16[32,2048]{1,0:T(8,128)(2,1)S(1)} %copy-done.4), custom_call_target="tpu_custom_call" | custom-call | tf_op jit(solution)/shard_map/dw/pallas_call | solution.py:301
Async XLA Ops:
  38.8 1.2 %copy-start = (bf16[256,2048]{1,0:T(8,128)(2,1)S(1)}, bf16[256,2048]{1,0:T(8,128)(2,1)}, u32[]{:S(2)}) copy-start(bf16[256,2048]{1,0:T(8,128)(2,1)} %get-tuple-element.11.xb) | copy-start | bytes 3145732
  40.0 1.2 %copy-start.1 = (bf16[256,2048]{1,0:T(8,128)(2,1)S(1)}, bf16[256,2048]{1,0:T(8,128)(2,1)}, u32[]{:S(2)}) copy-start(bf16[256,2048]{1,0:T(8,128)(2,1)} %get-tuple-element.14.y) | copy-start | bytes 3145732
  41.2 1.0 %copy-start.2 = (bf16[256,1024]{1,0:T(8,128)(2,1)S(1)}, bf16[256,1024]{1,0:T(8,128)(2,1)}, u32[]{:S(2)}) copy-start(bf16[256,1024]{1,0:T(8,128)(2,1)} %get-tuple-element.13.zb) | copy-start | bytes 1572868
  42.3 1.0 %copy-start.3 = (bf16[256,1024]{1,0:T(8,128)(2,1)S(1)}, bf16[256,1024]{1,0:T(8,128)(2,1)}, u32[]{:S(2)}) copy-start(bf16[256,1024]{1,0:T(8,128)(2,1)} %get-tuple-element.12.dz) | copy-start | bytes 1572868
  43.3 0.9 %copy-start.4 = (bf16[32,2048]{1,0:T(8,128)(2,1)S(1)}, bf16[32,2048]{1,0:T(8,128)(2,1)}, u32[]{:S(2)}) copy-start(bf16[32,2048]{1,0:T(8,128)(2,1)} %get-tuple-element.15.dxi) | copy-start | bytes 393220

commit v2 on v1

--- a/solution.py
+++ b/solution.py
@@ -34,9 +34,9 @@
 
 
 def _gather_kernel(rows, x_hbm, y_hbm, w1_hbm, w2_hbm,
-                   xo, yo, zo, dzo, dx_ref,
-                   xg, yg, zs, dzs, g1s, w1, w2, w1t, w2t, pdx, psend, precv, rsend, rrecv,
-                   in_sem, w_sem, out_sem, ag_send, ag_recv, ag_precv,
+                   xg, yg, zs, dzs, dx_ref,
+                   g1s, w1, w2, w1t, w2t, pdx, psend, precv, rsend, rrecv,
+                   in_sem, w_sem, ag_send, ag_recv, ag_precv,
                    p_send, p_recv, r_send, r_recv):
     t = lax.axis_index('tp')
     z, c = t // 2, t % 2
@@ -206,18 +206,10 @@
     rs_start(2)
     arrivals(X, 3)
     partner_wait(X, 3)
-    xout = pltpu.make_async_copy(xg, xo, out_sem.at[0])
-    xout.start()
     step_u(3 * chunk, chunk)
-    zout = pltpu.make_async_copy(zs, zo, out_sem.at[1])
-    zout.start()
     arrivals(Y, 3)
     partner_wait(Y, 3)
-    yout = pltpu.make_async_copy(yg, yo, out_sem.at[2])
-    yout.start()
     step_g(3 * chunk, chunk)
-    dzout = pltpu.make_async_copy(dzs, dzo, out_sem.at[3])
-    dzout.start()
     step_dx(3 * chunk, chunk)
     pair_start(3)
     rs_start(3)
@@ -254,8 +246,6 @@
         pair_copy(k).wait_send()
     for k in (1, 2, 3):
         rs_copy(k).wait_send()
-    for cp in (xout, yout, zout, dzout):
-        cp.wait()
 
 
 def _dw_kernel(xb, dz, zb, y, dxi, dw1, dw2, dx):
@@ -275,27 +265,25 @@
         n = 8 * rows
         vm = pltpu.VMEM
         sem = pltpu.SemaphoreType.DMA
-        anyspec = pl.BlockSpec(memory_space=pl.ANY)
+        vspec = pl.BlockSpec(memory_space=vm)
+        hbm = pl.BlockSpec(memory_space=pltpu.HBM)
         xg, yg, zg, dzg, dx = pl.pallas_call(
             lambda *refs: _gather_kernel(rows, *refs),
-            out_shape=(
-                jax.ShapeDtypeStruct((n, h), BF16), jax.ShapeDtypeStruct((n, h), BF16),
-                jax.ShapeDtypeStruct((n, f), BF16), jax.ShapeDtypeStruct((n, f), BF16),
-                jax.ShapeDtypeStruct((rows, h), BF16)),
-            in_specs=[anyspec] * 4,
-            out_specs=(anyspec,) * 4 + (pl.BlockSpec(memory_space=pltpu.VMEM),),
+            out_shape=(vm((n, h), BF16), vm((n, h), BF16), vm((n, f), BF16), vm((n, f), BF16), vm((rows, h), BF16)),
+            in_specs=[hbm] * 4,
+            out_specs=(vspec,) * 5,
             scratch_shapes=[
-                vm((n, h), BF16), vm((n, h), BF16), vm((n, f), BF16), vm((n, f), BF16), vm((n, f), F32),
+                vm((n, f), F32),
                 vm((h, f), BF16), vm((f, h), BF16), vm((f, h), BF16), vm((h, f), BF16),
                 vm((n, h), F32), vm((4, rows, h), BF16), vm((4, rows, h), BF16),
                 vm((4, rows, h), BF16), vm((4, rows, h), BF16),
-                sem((2,)), sem((2,)), sem((4,)), sem((3, 2, 4)), sem((2, 4)), sem((2, 4)),
+                sem((2,)), sem((2,)), sem((3, 2, 4)), sem((2, 4)), sem((2, 4)),
                 sem((4,)), sem((4,)), sem((4,)), sem((4,)),
             ],
             compiler_params=pltpu.CompilerParams(
-                collective_id=0, has_side_effects=True, vmem_limit_bytes=56 * MIB),
+                collective_id=0, has_side_effects=True, vmem_limit_bytes=40 * MIB),
             name='gather_dx',
-        )(x, dy, w1, w2)
+        )(*(pltpu.with_memory_space_constraint(a, pltpu.HBM) for a in (x, dy, w1, w2)))
         steps = 8
         hb, fb = h // steps, f // steps
         dw1, dw2, dx = pl.pallas_call(

time: 52.4 us -> 46.1 us (0.88)
  local copies, waits for them, and re-layouts: 5.43 us -> 0 us
  Pallas kernels: 46 us -> 45.4 us
    unnamed x10 -> x0, local copies, waits for them, and re-layouts: 5.43 us -> none
    pallas_call x1, Pallas kernels: 38.2 us -> 37.5 us  [body(): pl.pallas_call(lambda *refs: _gather_kernel(rows, *refs), out_shape=(vm((...]
where the time goes in v2:
time: 46.1 us; the launch traced here: 46 us
  Pallas kernels  45.4 us (98%)
  between operations  0.64 us (1%)
    pallas_call x1, Pallas kernels, body(): pl.pallas_call(lambda *refs: _gather_kernel(rows, *refs), out_shape=(vm((...  37.5 us
    pallas_call x1, Pallas kernels, body(): pl.pallas_call(_dw_kernel, grid=(steps,), out_shape=(jax.ShapeDtypeStruct...  7.9 us

profile of v2, /device:TPU:0, one launch (start us, length us, event | category | flops | bytes accessed | tf_op | source)
XLA Modules:
  0.0 46.0 jit_solution(15048296427472273147)
XLA Ops:
  0.6 37.5 %gather_dx.1 = (bf16[256,2048]{1,0:T(8,128)(2,1)S(1)}, bf16[256,2048]{1,0:T(8,128)(2,1)S(1)}, bf16[256,1024]{1,0:T(8,128)(2,1)S(1)}, bf16[256,1024]{1,0:T(8,128)(2,1)S(1)}, bf16[32,2048]{1,0:T(8,128)(2,1)S(1)}) custom-call(bf16[32,2048]{1,0:T(8,128)(2,1)} %refs_0_.1, bf16[32,2048]{1,0:T(8,128)(2,1)} %refs_1_.1, bf16[2048,1024]{1,0:T(8,128)(2,1)} %refs_2_.1, ...), custom_call_target="tpu_custom_call" | custom-call | tf_op jit(solution)/shard_map/gather_dx/pallas_call | solution.py:270
  38.1 7.9 %dw.1 = (f32[2048,1024]{1,0:T(8,128)}, f32[1024,2048]{1,0:T(8,128)}, bf16[32,2048]{1,0:T(8,128)(2,1)}) custom-call(bf16[256,2048]{1,0:T(8,128)(2,1)S(1)} %get-tuple-element.11.xb, bf16[256,1024]{1,0:T(8,128)(2,1)S(1)} %get-tuple-element.12.dz, bf16[256,1024]{1,0:T(8,128)(2,1)S(1)} %get-tuple-element.13.zb, bf16[256,2048]{1,0:T(8,128)(2,1)S(1)} %get-tuple-element.14.y, ...), custom_call_target="tpu_custom_call" | custom-call | tf_op jit(solution)/shard_map/dw/pallas_call | solution.py:289

commit v3 on v0

v3 whole, which is shorter than its diff:
```python
import math

import jax
import jax.numpy as jnp
from jax import lax
from jax.experimental import pallas as pl
from jax.experimental.pallas import tpu as pltpu
from jax.sharding import PartitionSpec as P


C0 = math.sqrt(2.0 / math.pi)
C1 = 0.044715
BF16 = jnp.bfloat16
F32 = jnp.float32
X, Y = 0, 1
MESH = pl.DeviceIdType.MESH
MIB = 1 << 20


def _gelu(u):
    t = jnp.tanh(C0 * (u + C1 * u * u * u))
    return 0.5 * u * (1.0 + t), 0.5 * (1.0 + t) + 0.5 * u * (1.0 - t * t) * C0 * (1.0 + 3.0 * C1 * u * u)


def _gather_kernel(rows, x_hbm, y_hbm, w1_hbm, w2_hbm,
                   xg, yg, zs, dzs, acc_ref, last_ref, mid_ref,
                   g1s, w1, w2, w1t, w2t, pdx, psend, precv, rsend, rrecv,
                   in_sem, w_sem, ag_send, ag_psend, ag_recv, ag_precv,
                   p_send, p_recv, r_send, r_recv):
    t = lax.axis_index('tp')
    z, c = t // 2, t % 2
    chunk = 2 * rows
    f, h = w2.shape
    low = z < 2
    near_end, near_mid = jnp.where(low, 0, 3), jnp.where(low, 1, 2)
    far_mid, far_end = 3 - near_mid, 3 - near_end
    is_end = z == near_end
    is_mid = jnp.logical_not(is_end)
    bufs = (xg, yg)

    def dev(chip, core):
        return {'tp': 2 * chip + core}

    def block(a, slot, core):
        return bufs[a].at[pl.ds(pl.multiple_of(slot * chunk + core * rows, rows), rows), :]

    loads = [pltpu.make_async_copy(src, block(a, 0, c), in_sem.at[a]) for a, src in ((X, x_hbm), (Y, y_hbm))]
    piece = 256
    w2loads = [(w2_hbm, w2, i) for i in range(f // piece)]
    w1loads = [(w1_hbm, w1, i) for i in range(h // piece)]

    def wload(src, dst, i, j):
        s = pl.ds(i * piece, piece)
        return pltpu.make_async_copy(src.at[s, :], dst.at[s, :], w_sem.at[j])

    wloads = [wload(*x, j) for j, x in enumerate(w2loads + w1loads)]
    for cp in loads:
        cp.start()

    barrier = pltpu.get_barrier_semaphore()

    def greet(chip, core):
        pl.semaphore_signal(barrier, inc=1, device_id=dev(chip, core), device_id_type=MESH)

    greet(z, 1 - c)

    @pl.when(is_end)
    def _():
        greet(near_mid, c)

    @pl.when(is_mid)
    def _():
        greet(near_end, c)
        greet(far_mid, c)
        greet(far_end, c)

    for cp in loads:
        cp.wait()
    for cp in wloads:
        cp.start()
    pl.semaphore_wait(barrier, 3)

    def ag_copy(a, i, slot, chip, to_slot):
        return pltpu.make_async_remote_copy(
            src_ref=block(a, slot, c), dst_ref=block(a, to_slot, c),
            send_sem=ag_send.at[a, i], recv_sem=ag_recv.at[a, to_slot],
            device_id=dev(chip, c), device_id_type=MESH)

    def share(a, slot):
        return pltpu.make_async_remote_copy(
            src_ref=block(a, slot, c), dst_ref=block(a, slot, c),
            send_sem=ag_psend.at[a, slot], recv_sem=ag_precv.at[a, slot],
            device_id=dev(z, 1 - c), device_id_type=MESH)

    def end_msg(a, i):
        return ag_copy(a, i, 0, *((far_mid, 1), (near_mid, 3))[i])

    def mid_msg(a, i):
        return ag_copy(a, i, *((0, near_end, 1), (0, far_mid, 2), (1, near_end, 2), (2, near_end, 3))[i])

    def arrive(a, slot, forward=None):
        dst = block(a, slot, c)
        pltpu.make_async_copy(dst, dst, ag_recv.at[a, slot]).wait()
        if forward is not None:
            mid_msg(a, forward).start()
        share(a, slot).start()

    def partner(a, slot):
        share(a, slot).wait_recv()

    def step_u(slot, m=1):
        r = pl.ds(slot * chunk, m * chunk)

        @pl.loop(0, f // 512)
        def _(n):
            s = pl.ds(pl.multiple_of(n * 512, 512), 512)
            u = jnp.dot(xg[r, :], w1[:, s], preferred_element_type=F32).astype(BF16)
            g0, g1 = _gelu(u.astype(F32))
            zs[r, s] = g0.astype(BF16)
            g1s[r, s] = g1

    def step_g(slot, m=1):
        r = pl.ds(slot * chunk, m * chunk)

        @pl.loop(0, f // 512)
        def _(n):
            s = pl.ds(pl.multiple_of(n * 512, 512), 512)
            g = jnp.dot(yg[r, :], w2t[:, s], preferred_element_type=F32)
            dzs[r, s] = (g * g1s[r, s]).astype(BF16)

    def step_dx(slot, m=1):
        r = pl.ds(slot * chunk, m * chunk)

        @pl.loop(0, h // 512)
        def _(n):
            s = pl.ds(pl.multiple_of(n * 512, 512), 512)
            pdx[r, s] = jnp.dot(dzs[r, :], w1t[:, s], preferred_element_type=F32)

        for k in range(slot, slot + m):
            psend[k] = part(k, 1 - c).astype(BF16)
            pair_copy(k).start()

    def part(k, core):
        return pdx[pl.ds(pl.multiple_of(k * chunk + core * rows, rows), rows), :]

    def pair_copy(k):
        return pltpu.make_async_remote_copy(
            src_ref=psend.at[k], dst_ref=precv.at[k], send_sem=p_send.at[k], recv_sem=p_recv.at[k],
            device_id=dev(z, 1 - c), device_id_type=MESH)

    def pair_sum(k):
        pair_copy(k).wait_recv()
        return part(k, c) + precv[k].astype(F32)

    def rs_copy(k, chip, i):
        return pltpu.make_async_remote_copy(
            src_ref=rsend.at[k], dst_ref=rrecv.at[i], send_sem=r_send.at[k], recv_sem=r_recv.at[i],
            device_id=dev(chip, c), device_id_type=MESH)

    def rs_recv(i):
        pltpu.make_async_copy(rrecv.at[i], rrecv.at[i], r_recv.at[i]).wait()
        return rrecv[i].astype(F32)

    @pl.when(is_end)
    def _():
        end_msg(X, 0).start()

    @pl.when(is_mid)
    def _():
        mid_msg(X, 0).start()

    share(X, 0).start()
    share(Y, 0).start()

    for i in range(f // piece):
        wloads[i].wait()
        w2t[:, i * piece:(i + 1) * piece] = w2[i * piece:(i + 1) * piece, :].T

    @pl.when(is_end)
    def _():
        end_msg(Y, 0).start()

    @pl.when(is_mid)
    def _():
        mid_msg(Y, 0).start()

    for i in range(h // piece):
        wloads[f // piece + i].wait()
        w1t[:, i * piece:(i + 1) * piece] = w1[i * piece:(i + 1) * piece, :].T

    @pl.when(is_end)
    def _():
        partner(X, 0)
        arrive(X, 1)
        end_msg(X, 1).start()
        partner(X, 1)
        step_u(0, 2)
        end_msg(Y, 1).start()
        arrive(Y, 1)
        partner(Y, 0)
        partner(Y, 1)
        step_g(0, 2)
        step_dx(0, 2)
        arrive(X, 2)
        partner(X, 2)
        step_u(2)
        arrive(Y, 2)
        acc_ref[...] = pair_sum(0)
        rsend[1] = pair_sum(1).astype(BF16)
        rs_copy(1, near_mid, 0).start()
        partner(Y, 2)
        step_g(2)
        arrive(X, 3)
        step_dx(2)
        partner(X, 3)
        rsend[2] = pair_sum(2).astype(BF16)
        rs_copy(2, far_end, 0).start()
        step_u(3)
        arrive(Y, 3)
        partner(Y, 3)
        step_g(3)
        step_dx(3)
        last_ref[...] = pair_sum(3).astype(BF16)
        mid_ref[...] = jnp.zeros_like(mid_ref)
        acc_ref[...] += rs_recv(0)
        for a in (X, Y):
            end_msg(a, 0).wait_send()
            end_msg(a, 1).wait_send()
        rs_copy(1, near_mid, 0).wait_send()
        rs_copy(2, far_end, 0).wait_send()

    @pl.when(is_mid)
    def _():
        partner(X, 0)
        arrive(X, 1, forward=2)
        mid_msg(X, 1).start()
        partner(X, 1)
        step_u(0, 2)
        mid_msg(Y, 1).start()
        arrive(Y, 1, forward=2)
        partner(Y, 0)
        partner(Y, 1)
        step_g(0, 2)
        arrive(X, 2, forward=3)
        arrive(X, 3)
        step_dx(0, 2)
        arrive(Y, 2, forward=3)
        partner(X, 2)
        partner(X, 3)
        step_u(2, 2)
        arrive(Y, 3)
        acc_ref[...] = pair_sum(0)
        rsend[1] = pair_sum(1).astype(BF16)
        rs_copy(1, far_mid, 1).start()
        partner(Y, 2)
        partner(Y, 3)
        step_g(2, 2)
        step_dx(2, 2)
        mid_ref[...] = pair_sum(2).astype(BF16)
        last_ref[...] = (pair_sum(3) + rs_recv(1)).astype(BF16)
        acc_ref[...] += rs_recv(0)
        for a in (X, Y):
            for i in range(4):
                mid_msg(a, i).wait_send()
        rs_copy(1, far_mid, 1).wait_send()

    for a in (X, Y):
        for k in range(4):
            share(a, k).wait_send()
    for k in range(4):
        pair_copy(k).wait_send()


def _dw_kernel(x, dz, zz, y, dw1, dw2, b1, b2, sem):
    dims = (((0,), (0,)), ((), ()))
    n = sem.shape[1]
    hb, fb = x.shape[1] // n, zz.shape[1] // n

    def out(j, i):
        src, dst, m = ((b1, dw1, hb), (b2, dw2, fb))[j]
        s = pl.ds(i * m, m)
        return pltpu.make_async_copy(src.at[s, :], dst.at[s, :], sem.at[j, i])

    for i in range(n):
        b1[pl.ds(i * hb, hb), :] = lax.dot_general(
            x[:, pl.ds(i * hb, hb)], dz[...], dims, preferred_element_type=F32)
        out(0, i).start()
        b2[pl.ds(i * fb, fb), :] = lax.dot_general(
            zz[:, pl.ds(i * fb, fb)], y[...], dims, preferred_element_type=F32)
        out(1, i).start()
    for i in range(n):
        out(0, i).wait()
        out(1, i).wait()


def solution(mesh):
    def body(x, dy, w1, w2):
        rows, h = x.shape
        f = w1.shape[1]
        n = 8 * rows
        vm = pltpu.VMEM
        sem = pltpu.SemaphoreType.DMA
        vspec = pl.BlockSpec(memory_space=vm)
        hbm = pl.BlockSpec(memory_space=pltpu.HBM)
        xg, yg, zg, dzg, acc, last, mid = pl.pallas_call(
            lambda *refs: _gather_kernel(rows, *refs),
            out_shape=(vm((n, h), BF16), vm((n, h), BF16), vm((n, f), BF16), vm((n, f), BF16),
                       vm((rows, h), F32), vm((rows, h), BF16), vm((rows, h), BF16)),
            in_specs=[hbm] * 4,
            out_specs=(vspec,) * 7,
            scratch_shapes=[
                vm((n, f), F32),
                vm((h, f), BF16), vm((f, h), BF16), vm((f, h), BF16), vm((h, f), BF16),
                vm((n, h), F32), vm((4, rows, h), BF16), vm((4, rows, h), BF16),
                vm((3, rows, h), BF16), vm((2, rows, h), BF16),
                sem((2,)), sem(((f + h) // 256,)), sem((2, 4)), sem((2, 4)), sem((2, 4)), sem((2, 4)),
                sem((4,)), sem((4,)), sem((3,)), sem((2,)),
            ],
            compiler_params=pltpu.CompilerParams(
                collective_id=0, has_side_effects=True, vmem_limit_bytes=40 * MIB),
            name='gather_dx',
        )(*(pltpu.with_memory_space_constraint(a, pltpu.HBM) for a in (x, dy, w1, w2)))
        mid = lax.ppermute(mid, 'tp', [(2, 4), (3, 5), (4, 2), (5, 3)])
        hops = ((0, 2), (2, 3), (3, 1), (1, 0))
        far = lax.ppermute(last, 'tp', [(2 * a + c, 2 * b + c) for a, b in hops for c in (0, 1)])
        steps = 8
        dw1, dw2 = pl.pallas_call(
            _dw_kernel,
            out_shape=(jax.ShapeDtypeStruct((h, f), F32), jax.ShapeDtypeStruct((f, h), F32)),
            in_specs=[vspec] * 4,
            out_specs=(hbm,) * 2,
            scratch_shapes=[vm((h, f), F32), vm((f, h), F32), sem((2, steps))],
            compiler_params=pltpu.CompilerParams(vmem_limit_bytes=24 * MIB),
            cost_estimate=pl.CostEstimate(
                flops=4 * n * h * f, bytes_accessed=8 * h * f, transcendentals=0),
            name='dw',
        )(xg, dzg, zg, yg)
        dx = (acc + far.astype(F32) + mid.astype(F32)).astype(BF16)
        return dx, dw1, dw2

    return jax.shard_map(
        body, mesh=mesh,
        in_specs=(P(('dp', 'tp'), None), P(('dp', 'tp'), None), P(None, 'tp'), P('tp', None)),
        out_specs=(P(('dp', 'tp'), None), P('dp', 'tp'), P(('dp', 'tp'), None)),
        check_vma=False)
```

time: 110 us -> 38.5 us (0.35)
  the two profiles are of different devices: /device:TPU:0 before, /device:TPU:13 now
where the time goes in v3:
time: 38.5 us; the launch traced here: 38.4 us
  Pallas kernels  28.4 us (74%)
  starting transfers between devices  8.58 us (22%)
  other arithmetic  0.7 us (2%)
  between operations  0.67 us (2%)
    pallas_call x1, Pallas kernels, body(): pl.pallas_call(lambda *refs: _gather_kernel(rows, *refs), out_shape=(vm((...  22.2 us
    pallas_call x1, Pallas kernels, body(): pl.pallas_call(_dw_kernel, out_shape=(jax.ShapeDtypeStruct((h, f), F32),...  6.29 us
    ppermute x1, starting transfers between devices, body(): lax.ppermute(last, 'tp', [(2 * a + c, 2 * b + c) for a, b in hops for c i...  5.49 us
    ppermute x1, starting transfers between devices, body(): mid = lax.ppermute(mid, 'tp', [(2, 4), (3, 5), (4, 2), (5, 3)])  3.08 us
  transfers between devices with their start and end apart: 2, of which 0 were waited for; matrix products, arithmetic and copies ran while one was open for 0% of the time, Pallas kernels for 16%

profile of v3, /device:TPU:13, one launch (start us, length us, event | category | flops | bytes accessed | tf_op | source)
XLA Modules:
  0.0 38.4 jit_solution(4637646939046699037)
XLA Ops:
  0.6 22.2 %gather_dx.1 = (bf16[256,2048]{1,0:T(8,128)(2,1)S(1)}, bf16[256,2048]{1,0:T(8,128)(2,1)S(1)}, bf16[256,1024]{1,0:T(8,128)(2,1)S(1)}, bf16[256,1024]{1,0:T(8,128)...) custom-call(bf16[32,2048]{1,0:T(8,128)(2,1)} %refs_0_.1, ...), custom_call_target="tpu_custom_call" | custom-call | tf_op jit(solution)/shard_map/gather_dx/pallas_call | solution.py:305
  22.8 5.5 %collective-permute-start = (bf16[32,2048]{1,0:T(8,128)(2,1)S(1)}, bf16[32,2048]{1,0:T(8,128)(2,1)S(1)}, u32[]{:S(2)}, u32[]{:S(2)}) collective-permute-start(bf16[32,2048]{1,0:T(8,128)(2,1)S(1)} %get-tuple-element.13), channel_id=1, source_target_pairs={{0,4},{1,5},{4,6},{5,7},{6,2},{7,3},{2,0},{3,1},{8,12},{9,13},{12,... | collective-permute-start | bytes 393224 | tf_op jit(solution)/shard_map/ppermute | solution.py:325
  28.3 3.1 %collective-permute-start.1 = (bf16[32,2048]{1,0:T(8,128)(2,1)S(1)}, bf16[32,2048]{1,0:T(8,128)(2,1)S(1)}, u32[]{:S(2)}, u32[]{:S(2)}) collective-permute-start(bf16[32,2048]{1,0:T(8,128)(2,1)S(1)} %get-tuple-element.14), channel_id=1, source_target_pairs={{2,4},{3,5},{4,2},{5,3},{10,12},{11,13},{12,10},{13,11},{18,20},{1... | collective-permute-start | bytes 393224 | tf_op jit(solution)/shard_map/ppermute | solution.py:323
  31.4 6.3 %dw.1 = (f32[2048,1024]{1,0:T(8,128)}, f32[1024,2048]{1,0:T(8,128)}) custom-call(bf16[256,2048]{1,0:T(8,128)(2,1)S(1)} %get-tuple-element.15.x, bf16[256,1024]{1,0:T(8,128)(2,1)S(1)} %get-tuple-element.16.dz, bf16[256,1024]{1,0:T(8,128)(2,1)S(1)} %get-tuple-element.17.zz, bf16[256,2048]{1,0:T(8,128)(2,1)S(1)} %get-tuple-element.18.y), custom_call_target="tpu_custom_call" | custom-call | flops 2147483648 | bytes 16777216 | tf_op jit(solution)/shard_map/dw/pallas_call | solution.py:327
  37.7 0.0 collective-permute-done
  37.7 0.0 collective-permute-done.1
  37.7 0.7 %add_convert_fusion = bf16[32,2048]{1,0:T(8,128)(2,1)} fusion(bf16[32,2048]{1,0:T(8,128)(2,1)S(1)} %collective-permute-done.1, f32[32,2048]{1,0:T(8,128)S(1)} %get-tuple-element.12, bf16[32,2048]{1,0:T(8,128)(2,1)S(1)} %collective-permute-done), kind=kLoop, calls=%fused_computation | loop fusion | flops 327680 | bytes 655360 | tf_op jit(solution)/shard_map/convert_element_type | solution.py:338
Async XLA Ops:
  22.8 14.9 %collective-permute-start = (bf16[32,2048]{1,0:T(8,128)(2,1)S(1)}, bf16[32,2048]{1,0:T(8,128)(2,1)S(1)}, u32[]{:S(2)}, u32[]{:S(2)}) collective-permute-start(bf16[32,2048]{1,0:T(8,128)(2,1)S(1)} %get-tuple-element.13), channel_id=1, source_target_pairs={{0,4},{1,5},{4,6},{5,7},{6,2},{7,3},{2,0},{3,1},{8,12},{9,13},{12,... | collective-permute-start | bytes 393224 | tf_op jit(solution)/shard_map/ppermute | solution.py:325
  28.3 9.4 %collective-permute-start.1 = (bf16[32,2048]{1,0:T(8,128)(2,1)S(1)}, bf16[32,2048]{1,0:T(8,128)(2,1)S(1)}, u32[]{:S(2)}, u32[]{:S(2)}) collective-permute-start(bf16[32,2048]{1,0:T(8,128)(2,1)S(1)} %get-tuple-element.14), channel_id=1, source_target_pairs={{2,4},{3,5},{4,2},{5,3},{10,12},{11,13},{12,10},{13,11},{18,20},{1... | collective-permute-start | bytes 393224 | tf_op jit(solution)/shard_map/ppermute | solution.py:323

commit v4 on v3

--- a/solution.py
+++ b/solution.py
@@ -12,7 +12,7 @@
 C1 = 0.044715
 BF16 = jnp.bfloat16
 F32 = jnp.float32
-X, Y = 0, 1
+X, Y, Y0, Y1 = range(4)
 MESH = pl.DeviceIdType.MESH
 MIB = 1 << 20
 
@@ -25,8 +25,7 @@
 def _gather_kernel(rows, x_hbm, y_hbm, w1_hbm, w2_hbm,
                    xg, yg, zs, dzs, acc_ref, last_ref, mid_ref,
                    g1s, w1, w2, w1t, w2t, pdx, psend, precv, rsend, rrecv,
-                   in_sem, w_sem, ag_send, ag_psend, ag_recv, ag_precv,
-                   p_send, p_recv, r_send, r_recv):
+                   in_sem, w_sem, ag_send, ag_recv, ag_precv, p_recv, r_recv):
     t = lax.axis_index('tp')
     z, c = t // 2, t % 2
     chunk = 2 * rows
@@ -36,13 +35,18 @@
     far_mid, far_end = 3 - near_mid, 3 - near_end
     is_end = z == near_end
     is_mid = jnp.logical_not(is_end)
-    bufs = (xg, yg)
 
     def dev(chip, core):
         return {'tp': 2 * chip + core}
 
     def block(a, slot, core):
-        return bufs[a].at[pl.ds(pl.multiple_of(slot * chunk + core * rows, rows), rows), :]
+        r = pl.ds(pl.multiple_of(slot * chunk + core * rows, rows), rows)
+        if a in (X, Y):
+            return (xg, yg)[a].at[r, :]
+        return yg.at[r, pl.ds((a - Y0) * (h // 2), h // 2)]
+
+    def flag(a):
+        return {X: 0, Y: 1, Y0: 1, Y1: 2}[a]
 
     loads = [pltpu.make_async_copy(src, block(a, 0, c), in_sem.at[a]) for a, src in ((X, x_hbm), (Y, y_hbm))]
     piece = 256
@@ -80,27 +84,27 @@
         cp.start()
     pl.semaphore_wait(barrier, 3)
 
-    def ag_copy(a, i, slot, chip, to_slot):
+    def ag_copy(a, slot, chip, to_slot):
         return pltpu.make_async_remote_copy(
             src_ref=block(a, slot, c), dst_ref=block(a, to_slot, c),
-            send_sem=ag_send.at[a, i], recv_sem=ag_recv.at[a, to_slot],
+            send_sem=ag_send, recv_sem=ag_recv.at[flag(a), to_slot],
             device_id=dev(chip, c), device_id_type=MESH)
 
     def share(a, slot):
         return pltpu.make_async_remote_copy(
             src_ref=block(a, slot, c), dst_ref=block(a, slot, c),
-            send_sem=ag_psend.at[a, slot], recv_sem=ag_precv.at[a, slot],
+            send_sem=ag_send, recv_sem=ag_precv.at[flag(a), slot],
             device_id=dev(z, 1 - c), device_id_type=MESH)
 
     def end_msg(a, i):
-        return ag_copy(a, i, 0, *((far_mid, 1), (near_mid, 3))[i])
+        return ag_copy(a, 0, *((far_mid, 1), (near_mid, 3))[i])
 
     def mid_msg(a, i):
-        return ag_copy(a, i, *((0, near_end, 1), (0, far_mid, 2), (1, near_end, 2), (2, near_end, 3))[i])
+        return ag_copy(a, *((0, near_end, 1), (0, far_mid, 2), (1, near_end, 2), (2, near_end, 3))[i])
 
     def arrive(a, slot, forward=None):
         dst = block(a, slot, c)
-        pltpu.make_async_copy(dst, dst, ag_recv.at[a, slot]).wait()
+        pltpu.make_async_copy(dst, dst, ag_recv.at[flag(a), slot]).wait()
         if forward is not None:
             mid_msg(a, forward).start()
         share(a, slot).start()
@@ -128,38 +132,64 @@
             g = jnp.dot(yg[r, :], w2t[:, s], preferred_element_type=F32)
             dzs[r, s] = (g * g1s[r, s]).astype(BF16)
 
-    def step_dx(slot, m=1):
-        r = pl.ds(slot * chunk, m * chunk)
-
-        @pl.loop(0, h // 512)
+    def half_g(slot, i):
+        r = pl.ds(slot * chunk, chunk)
+        kk = pl.ds(i * (h // 2), h // 2)
+
+        @pl.loop(0, f // 512)
         def _(n):
             s = pl.ds(pl.multiple_of(n * 512, 512), 512)
+            g = jnp.dot(yg[r, kk], w2t[kk, s], preferred_element_type=F32)
+            if i == 0:
+                pdx[r, s] = g
+            else:
+                dzs[r, s] = ((g + pdx[r, s]) * g1s[r, s]).astype(BF16)
+
+    def step_dx(slot, m=1, half=None):
+        r = pl.ds(slot * chunk, m * chunk)
+        per = h // 512 if half is None else h // 1024
+
+        @pl.loop(0, per)
+        def _(n):
+            s = pl.ds(pl.multiple_of(((half or 0) * per + n) * 512, 512), 512)
             pdx[r, s] = jnp.dot(dzs[r, :], w1t[:, s], preferred_element_type=F32)
-
-        for k in range(slot, slot + m):
-            psend[k] = part(k, 1 - c).astype(BF16)
-            pair_copy(k).start()
-
-    def part(k, core):
-        return pdx[pl.ds(pl.multiple_of(k * chunk + core * rows, rows), rows), :]
-
-    def pair_copy(k):
+            for k in range(slot, slot + m):
+                psend[k, :, s] = part(k, 1 - c, s).astype(BF16)
+                pair_copy(k, s, half).start()
+
+    def part(k, core, s=slice(None)):
+        return pdx[pl.ds(pl.multiple_of(k * chunk + core * rows, rows), rows), s]
+
+    def cols(half):
+        return slice(None) if half is None else pl.ds(half * (h // 2), h // 2)
+
+    def pair_copy(k, s, half=None):
         return pltpu.make_async_remote_copy(
-            src_ref=psend.at[k], dst_ref=precv.at[k], send_sem=p_send.at[k], recv_sem=p_recv.at[k],
+            src_ref=psend.at[k, :, s], dst_ref=precv.at[k, :, s], send_sem=ag_send,
+            recv_sem=p_recv.at[4 if half == 1 else k],
             device_id=dev(z, 1 - c), device_id_type=MESH)
 
-    def pair_sum(k):
-        pair_copy(k).wait_recv()
-        return part(k, c) + precv[k].astype(F32)
-
-    def rs_copy(k, chip, i):
+    def pair_sum(k, half=None):
+        s = cols(half)
+        pair_copy(k, s, half).wait_recv()
+        return part(k, c, s) + precv[k, :, s].astype(F32)
+
+    def rs_copy(k, chip, i, half=None):
+        s = cols(half)
         return pltpu.make_async_remote_copy(
-            src_ref=rsend.at[k], dst_ref=rrecv.at[i], send_sem=r_send.at[k], recv_sem=r_recv.at[i],
+            src_ref=rsend.at[k, :, s], dst_ref=rrecv.at[i, :, s], send_sem=ag_send,
+            recv_sem=r_recv.at[2 if half == 1 else i],
             device_id=dev(chip, c), device_id_type=MESH)
 
-    def rs_recv(i):
-        pltpu.make_async_copy(rrecv.at[i], rrecv.at[i], r_recv.at[i]).wait()
-        return rrecv[i].astype(F32)
+    def rs_recv(i, half=None):
+        s = cols(half)
+        dst = rrecv.at[i, :, s]
+        pltpu.make_async_copy(dst, dst, r_recv.at[2 if half == 1 else i]).wait()
+        return rrecv[i, :, s].astype(F32)
+
+    def drain(n):
+        for r in (xg, yg, xg.at[pl.ds(0, (n + 12 - 16) * rows), :]):
+            pltpu.make_async_copy(r, r, ag_send).wait()
 
     @pl.when(is_end)
     def _():
@@ -192,14 +222,14 @@
     def _():
         partner(X, 0)
         arrive(X, 1)
-        end_msg(X, 1).start()
         partner(X, 1)
         step_u(0, 2)
-        end_msg(Y, 1).start()
+        end_msg(X, 1).start()
         arrive(Y, 1)
         partner(Y, 0)
         partner(Y, 1)
         step_g(0, 2)
+        end_msg(Y, 1).start()
         step_dx(0, 2)
         arrive(X, 2)
         partner(X, 2)
@@ -210,65 +240,61 @@
         rs_copy(1, near_mid, 0).start()
         partner(Y, 2)
         step_g(2)
+        for i in (0, 1):
+            step_dx(2, half=i)
         arrive(X, 3)
-        step_dx(2)
+        for i in (0, 1):
+            rsend[2, :, cols(i)] = pair_sum(2, i).astype(BF16)
+            rs_copy(2, far_end, 0, i).start()
+        arrive(Y0, 3)
         partner(X, 3)
-        rsend[2] = pair_sum(2).astype(BF16)
-        rs_copy(2, far_end, 0).start()
         step_u(3)
-        arrive(Y, 3)
-        partner(Y, 3)
-        step_g(3)
+        arrive(Y1, 3)
+        partner(Y0, 3)
+        half_g(3, 0)
+        partner(Y1, 3)
+        half_g(3, 1)
         step_dx(3)
+        mid_ref[...] = jnp.zeros_like(mid_ref)
         last_ref[...] = pair_sum(3).astype(BF16)
-        mid_ref[...] = jnp.zeros_like(mid_ref)
-        acc_ref[...] += rs_recv(0)
-        for a in (X, Y):
-            end_msg(a, 0).wait_send()
-            end_msg(a, 1).wait_send()
-        rs_copy(1, near_mid, 0).wait_send()
-        rs_copy(2, far_end, 0).wait_send()
+        for i in (0, 1):
+            acc_ref[:, cols(i)] += rs_recv(0, i)
+        drain(4 + 2)
 
     @pl.when(is_mid)
     def _():
         partner(X, 0)
         arrive(X, 1, forward=2)
+        partner(X, 1)
         mid_msg(X, 1).start()
-        partner(X, 1)
         step_u(0, 2)
-        mid_msg(Y, 1).start()
+        mid_msg(Y0, 1).start()
         arrive(Y, 1, forward=2)
         partner(Y, 0)
         partner(Y, 1)
+        mid_msg(Y1, 1).start()
         step_g(0, 2)
+        step_dx(0, 2)
         arrive(X, 2, forward=3)
         arrive(X, 3)
-        step_dx(0, 2)
-        arrive(Y, 2, forward=3)
+        arrive(Y0, 2, forward=3)
+        acc_ref[...] = pair_sum(0)
+        arrive(Y1, 2, forward=3)
+        rsend[1] = pair_sum(1).astype(BF16)
+        rs_copy(1, far_mid, 1).start()
         partner(X, 2)
         partner(X, 3)
         step_u(2, 2)
         arrive(Y, 3)
-        acc_ref[...] = pair_sum(0)
-        rsend[1] = pair_sum(1).astype(BF16)
-        rs_copy(1, far_mid, 1).start()
-        partner(Y, 2)
+        partner(Y0, 2)
+        partner(Y1, 2)
         partner(Y, 3)
         step_g(2, 2)
         step_dx(2, 2)
         mid_ref[...] = pair_sum(2).astype(BF16)
         last_ref[...] = (pair_sum(3) + rs_recv(1)).astype(BF16)
         acc_ref[...] += rs_recv(0)
-        for a in (X, Y):
-            for i in range(4):
-                mid_msg(a, i).wait_send()
-        rs_copy(1, far_mid, 1).wait_send()
-
-    for a in (X, Y):
-        for k in range(4):
-            share(a, k).wait_send()
-    for k in range(4):
-        pair_copy(k).wait_send()
+        drain(8 + 1)
 
 
 def _dw_kernel(x, dz, zz, y, dw1, dw2, b1, b2, sem):
@@ -313,14 +339,13 @@
                 vm((h, f), BF16), vm((f, h), BF16), vm((f, h), BF16), vm((h, f), BF16),
                 vm((n, h), F32), vm((4, rows, h), BF16), vm((4, rows, h), BF16),
                 vm((3, rows, h), BF16), vm((2, rows, h), BF16),
-                sem((2,)), sem(((f + h) // 256,)), sem((2, 4)), sem((2, 4)), sem((2, 4)), sem((2, 4)),
-                sem((4,)), sem((4,)), sem((3,)), sem((2,)),
+                sem((2,)), sem(((f + h) // 256,)), sem(()), sem((3, 4)), sem((3, 4)), sem((5,)), sem((3,)),
             ],
             compiler_params=pltpu.CompilerParams(
                 collective_id=0, has_side_effects=True, vmem_limit_bytes=40 * MIB),
             name='gather_dx',
         )(*(pltpu.with_memory_space_constraint(a, pltpu.HBM) for a in (x, dy, w1, w2)))
-        mid = lax.ppermute(mid, 'tp', [(2, 4), (3, 5), (4, 2), (5, 3)])
+        mid = lax.ppermute(mid, 'tp', [(0, 1), (1, 0), (2, 4), (3, 5), (4, 2), (5, 3), (6, 7), (7, 6)])
         hops = ((0, 2), (2, 3), (3, 1), (1, 0))
         far = lax.ppermute(last, 'tp', [(2 * a + c, 2 * b + c) for a, b in hops for c in (0, 1)])
         steps = 8

time: 38.5 us -> 35.6 us (0.925)
  the two profiles are of different devices: /device:TPU:13 before, /device:TPU:0 now
where the time goes in v4:
time: 35.6 us; the launch traced here: 35.5 us
  Pallas kernels  33.6 us (94%)
  other arithmetic  0.7 us (2%)
  between operations  0.67 us (2%)
  starting transfers between devices  0.53 us (1%)
    pallas_call x1, Pallas kernels, body(): pl.pallas_call(lambda *refs: _gather_kernel(rows, *refs), out_shape=(vm((...  27.3 us
    pallas_call x1, Pallas kernels, body(): pl.pallas_call(_dw_kernel, out_shape=(jax.ShapeDtypeStruct((h, f), F32),...  6.29 us
  transfers between devices with their start and end apart: 2, of which 0 were waited for; matrix products, arithmetic and copies ran while one was open for 0% of the time, Pallas kernels for 18%

profile of v4, /device:TPU:0, one launch (start us, length us, event | category | flops | bytes accessed | tf_op | source)
XLA Modules:
  0.0 35.5 jit_solution(12995460340169526590)
XLA Ops:
  0.6 27.3 %gather_dx.1 = (bf16[256,2048]{1,0:T(8,128)(2,1)S(1)}, bf16[256,2048]{1,0:T(8,128)(2,1)S(1)}, bf16[256,1024]{1,0:T(8,128)(2,1)S(1)}, bf16[256,1024]{1,0:T(8,128)...) custom-call(bf16[32,2048]{1,0:T(8,128)(2,1)} %refs_0_.1, ...), custom_call_target="tpu_custom_call" | custom-call | tf_op jit(solution)/shard_map/gather_dx/pallas_call | solution.py:331
  27.9 0.1 collective-permute-start
  28.0 0.5 %collective-permute-start.1 = (bf16[32,2048]{1,0:T(8,128)(2,1)S(1)}, bf16[32,2048]{1,0:T(8,128)(2,1)S(1)}, u32[]{:S(2)}, u32[]{:S(2)}) collective-permute-start(bf16[32,2048]{1,0:T(8,128)(2,1)S(1)} %get-tuple-element.14), channel_id=1, source_target_pairs={{0,1},{1,0},{2,4},{3,5},{4,2},{5,3},{6,7},{7,6},{8,9},{9,8},{10,12... | collective-permute-start | bytes 393224 | tf_op jit(solution)/shard_map/ppermute | solution.py:348
  28.4 6.3 %dw.1 = (f32[2048,1024]{1,0:T(8,128)}, f32[1024,2048]{1,0:T(8,128)}) custom-call(bf16[256,2048]{1,0:T(8,128)(2,1)S(1)} %get-tuple-element.15.x, bf16[256,1024]{1,0:T(8,128)(2,1)S(1)} %get-tuple-element.16.dz, bf16[256,1024]{1,0:T(8,128)(2,1)S(1)} %get-tuple-element.17.zz, bf16[256,2048]{1,0:T(8,128)(2,1)S(1)} %get-tuple-element.18.y), custom_call_target="tpu_custom_call" | custom-call | flops 2147483648 | bytes 16777216 | tf_op jit(solution)/shard_map/dw/pallas_call | solution.py:352
  34.7 0.0 collective-permute-done
  34.8 0.0 collective-permute-done.1
  34.8 0.7 %add_convert_fusion = bf16[32,2048]{1,0:T(8,128)(2,1)} fusion(bf16[32,2048]{1,0:T(8,128)(2,1)S(1)} %collective-permute-done.1, f32[32,2048]{1,0:T(8,128)S(1)} %get-tuple-element.12, bf16[32,2048]{1,0:T(8,128)(2,1)S(1)} %collective-permute-done), kind=kLoop, calls=%fused_computation | loop fusion | flops 327680 | bytes 655360 | tf_op jit(solution)/shard_map/convert_element_type | solution.py:363
Async XLA Ops:
  27.9 6.8 %collective-permute-start = (bf16[32,2048]{1,0:T(8,128)(2,1)S(1)}, bf16[32,2048]{1,0:T(8,128)(2,1)S(1)}, u32[]{:S(2)}, u32[]{:S(2)}) collective-permute-start(bf16[32,2048]{1,0:T(8,128)(2,1)S(1)} %get-tuple-element.13), channel_id=1, source_target_pairs={{0,4},{1,5},{4,6},{5,7},{6,2},{7,3},{2,0},{3,1},{8,12},{9,13},{12,... | collective-permute-start | bytes 393224 | tf_op jit(solution)/shard_map/ppermute | solution.py:350
  28.0 6.8 %collective-permute-start.1 = (bf16[32,2048]{1,0:T(8,128)(2,1)S(1)}, bf16[32,2048]{1,0:T(8,128)(2,1)S(1)}, u32[]{:S(2)}, u32[]{:S(2)}) collective-permute-start(bf16[32,2048]{1,0:T(8,128)(2,1)S(1)} %get-tuple-element.14), channel_id=1, source_target_pairs={{0,1},{1,0},{2,4},{3,5},{4,2},{5,3},{6,7},{7,6},{8,9},{9,8},{10,12... | collective-permute-start | bytes 393224 | tf_op jit(solution)/shard_map/ppermute | solution.py:348

commit v5 on v4

--- a/solution.py
+++ b/solution.py
@@ -14,6 +14,7 @@
 F32 = jnp.float32
 X, Y, Y0, Y1 = range(4)
 MESH = pl.DeviceIdType.MESH
+TN = (((0,), (0,)), ((), ()))
 MIB = 1 << 20
 
 
@@ -23,9 +24,9 @@
 
 
 def _gather_kernel(rows, x_hbm, y_hbm, w1_hbm, w2_hbm,
-                   xg, yg, zs, dzs, acc_ref, last_ref, mid_ref,
+                   xg, yg, zs, dzs, acc_ref, last_ref, mid_ref, pre_ref,
                    g1s, w1, w2, w1t, w2t, pdx, psend, precv, rsend, rrecv,
-                   in_sem, w_sem, ag_send, ag_recv, ag_precv, p_recv, r_recv):
+                   in_sem, w_sem, ag_send, ag_recv, ag_precv, p_recv, r_recv, met):
     t = lax.axis_index('tp')
     z, c = t // 2, t % 2
     chunk = 2 * rows
@@ -45,19 +46,15 @@
             return (xg, yg)[a].at[r, :]
         return yg.at[r, pl.ds((a - Y0) * (h // 2), h // 2)]
 
-    def flag(a):
-        return {X: 0, Y: 1, Y0: 1, Y1: 2}[a]
+    def flag(a, slot):
+        return {X: slot, Y: 4 + slot, Y0: 4 + slot, Y1: 8}[a]
 
     loads = [pltpu.make_async_copy(src, block(a, 0, c), in_sem.at[a]) for a, src in ((X, x_hbm), (Y, y_hbm))]
-    piece = 256
-    w2loads = [(w2_hbm, w2, i) for i in range(f // piece)]
-    w1loads = [(w1_hbm, w1, i) for i in range(h // piece)]
-
-    def wload(src, dst, i, j):
-        s = pl.ds(i * piece, piece)
-        return pltpu.make_async_copy(src.at[s, :], dst.at[s, :], w_sem.at[j])
-
-    wloads = [wload(*x, j) for j, x in enumerate(w2loads + w1loads)]
+    wloads = []
+    for hbm, w, n in ((w2_hbm, w2, 4), (w1_hbm, w1, 2)):
+        for i in range(n):
+            r = pl.ds(i * (w.shape[0] // n), w.shape[0] // n)
+            wloads.append(pltpu.make_async_copy(hbm.at[r, :], w.at[r, :], w_sem.at[len(wloads)]))
     for cp in loads:
         cp.start()
 
@@ -75,25 +72,37 @@
     @pl.when(is_mid)
     def _():
         greet(near_end, c)
+        greet(far_end, c)
+
+    low_mid = z == 1
+
+    @pl.when(low_mid)
+    def _():
         greet(far_mid, c)
-        greet(far_end, c)
 
     for cp in loads:
         cp.wait()
     for cp in wloads:
         cp.start()
-    pl.semaphore_wait(barrier, 3)
+
+    @pl.when(low_mid)
+    def _():
+        pl.semaphore_wait(barrier, 2)
+
+    @pl.when(jnp.logical_not(low_mid))
+    def _():
+        pl.semaphore_wait(barrier, 3)
 
     def ag_copy(a, slot, chip, to_slot):
         return pltpu.make_async_remote_copy(
             src_ref=block(a, slot, c), dst_ref=block(a, to_slot, c),
-            send_sem=ag_send, recv_sem=ag_recv.at[flag(a), to_slot],
+            send_sem=ag_send, recv_sem=ag_recv.at[flag(a, to_slot) - 1],
             device_id=dev(chip, c), device_id_type=MESH)
 
     def share(a, slot):
         return pltpu.make_async_remote_copy(
             src_ref=block(a, slot, c), dst_ref=block(a, slot, c),
-            send_sem=ag_send, recv_sem=ag_precv.at[flag(a), slot],
+            send_sem=ag_send, recv_sem=ag_precv.at[flag(a, slot)],
             device_id=dev(z, 1 - c), device_id_type=MESH)
 
     def end_msg(a, i):
@@ -104,7 +113,7 @@
 
     def arrive(a, slot, forward=None):
         dst = block(a, slot, c)
-        pltpu.make_async_copy(dst, dst, ag_recv.at[flag(a), slot]).wait()
+        pltpu.make_async_copy(dst, dst, ag_recv.at[flag(a, slot) - 1]).wait()
         if forward is not None:
             mid_msg(a, forward).start()
         share(a, slot).start()
@@ -112,12 +121,13 @@
     def partner(a, slot):
         share(a, slot).wait_recv()
 
-    def step_u(slot, m=1):
+    def step_u(slot, m=1, half=None):
         r = pl.ds(slot * chunk, m * chunk)
-
-        @pl.loop(0, f // 512)
+        nb = f if half is None else f // 2
+
+        @pl.loop(half or 0, (half or 0) + 1)
         def _(n):
-            s = pl.ds(pl.multiple_of(n * 512, 512), 512)
+            s = pl.ds(pl.multiple_of(n * nb, nb), nb)
             u = jnp.dot(xg[r, :], w1[:, s], preferred_element_type=F32).astype(BF16)
             g0, g1 = _gelu(u.astype(F32))
             zs[r, s] = g0.astype(BF16)
@@ -126,9 +136,9 @@
     def step_g(slot, m=1):
         r = pl.ds(slot * chunk, m * chunk)
 
-        @pl.loop(0, f // 512)
+        @pl.loop(0, f // 1024)
         def _(n):
-            s = pl.ds(pl.multiple_of(n * 512, 512), 512)
+            s = pl.ds(pl.multiple_of(n * 1024, 1024), 1024)
             g = jnp.dot(yg[r, :], w2t[:, s], preferred_element_type=F32)
             dzs[r, s] = (g * g1s[r, s]).astype(BF16)
 
@@ -136,9 +146,9 @@
         r = pl.ds(slot * chunk, chunk)
         kk = pl.ds(i * (h // 2), h // 2)
 
-        @pl.loop(0, f // 512)
+        @pl.loop(0, f // 1024)
         def _(n):
-            s = pl.ds(pl.multiple_of(n * 512, 512), 512)
+            s = pl.ds(pl.multiple_of(n * 1024, 1024), 1024)
             g = jnp.dot(yg[r, kk], w2t[kk, s], preferred_element_type=F32)
             if i == 0:
                 pdx[r, s] = g
@@ -147,15 +157,21 @@
 
     def step_dx(slot, m=1, half=None):
         r = pl.ds(slot * chunk, m * chunk)
-        per = h // 512 if half is None else h // 1024
+        per = h // 1024 if half is None else h // 2048
 
         @pl.loop(0, per)
         def _(n):
-            s = pl.ds(pl.multiple_of(((half or 0) * per + n) * 512, 512), 512)
+            s = pl.ds(pl.multiple_of(((half or 0) * per + n) * 1024, 1024), 1024)
             pdx[r, s] = jnp.dot(dzs[r, :], w1t[:, s], preferred_element_type=F32)
             for k in range(slot, slot + m):
                 psend[k, :, s] = part(k, 1 - c, s).astype(BF16)
                 pair_copy(k, s, half).start()
+
+    def first_dw():
+        @pl.loop(0, pre_ref.shape[0] // 256)
+        def _(n):
+            s = pl.ds(pl.multiple_of(n * 256, 256), 256)
+            pre_ref[s, :] = lax.dot_general(xg[:, s], dzs[...], TN, preferred_element_type=F32)
 
     def part(k, core, s=slice(None)):
         return pdx[pl.ds(pl.multiple_of(k * chunk + core * rows, rows), rows), s]
@@ -199,12 +215,17 @@
     def _():
         mid_msg(X, 0).start()
 
+        @pl.when(jnp.logical_not(low_mid))
+        def _():
+            pl.semaphore_signal(met, inc=1, device_id=dev(far_mid, c), device_id_type=MESH)
+
     share(X, 0).start()
     share(Y, 0).start()
 
-    for i in range(f // piece):
+    for i in range(4):
         wloads[i].wait()
-        w2t[:, i * piece:(i + 1) * piece] = w2[i * piece:(i + 1) * piece, :].T
+        r = pl.ds(i * (f // 4), f // 4)
+        w2t[:, r] = w2[r, :].T
 
     @pl.when(is_end)
     def _():
@@ -214,9 +235,11 @@
     def _():
         mid_msg(Y, 0).start()
 
-    for i in range(h // piece):
-        wloads[f // piece + i].wait()
-        w1t[:, i * piece:(i + 1) * piece] = w1[i * piece:(i + 1) * piece, :].T
+    for i in range(8):
+        if i % 4 == 0:
+            wloads[4 + i // 4].wait()
+        r = pl.ds(i * (h // 8), h // 8)
+        w1t[:, r] = w1[r, :].T
 
     @pl.when(is_end)
     def _():
@@ -246,15 +269,30 @@
         for i in (0, 1):
             rsend[2, :, cols(i)] = pair_sum(2, i).astype(BF16)
             rs_copy(2, far_end, 0, i).start()
-        arrive(Y0, 3)
-        partner(X, 3)
-        step_u(3)
-        arrive(Y1, 3)
-        partner(Y0, 3)
-        half_g(3, 0)
+
+        @pl.when(c == 1)
+        def _():
+            arrive(Y0, 3)
+            partner(X, 3)
+            step_u(3, half=0)
+            arrive(Y1, 3)
+            step_u(3, half=1)
+            partner(Y0, 3)
+            half_g(3, 0)
+
+        @pl.when(c == 0)
+        def _():
+            partner(X, 3)
+            step_u(3)
+            arrive(Y0, 3)
+            partner(Y0, 3)
+            half_g(3, 0)
+            arrive(Y1, 3)
+
         partner(Y1, 3)
         half_g(3, 1)
         step_dx(3)
+        first_dw()
         mid_ref[...] = jnp.zeros_like(mid_ref)
         last_ref[...] = pair_sum(3).astype(BF16)
         for i in (0, 1):
@@ -264,24 +302,49 @@
     @pl.when(is_mid)
     def _():
         partner(X, 0)
+        step_u(0)
         arrive(X, 1, forward=2)
+
+        @pl.when(low_mid)
+        def _():
+            pl.semaphore_wait(met, 1)
+
+        mid_msg(X, 1).start()
+
+        @pl.when(low)
+        def _():
+            arrive(Y, 1, forward=2)
+            mid_msg(Y0, 1).start()
+
         partner(X, 1)
-        mid_msg(X, 1).start()
-        step_u(0, 2)
-        mid_msg(Y0, 1).start()
-        arrive(Y, 1, forward=2)
+        step_u(1)
+
+        @pl.when(jnp.logical_not(low))
+        def _():
+            mid_msg(Y0, 1).start()
+            arrive(Y, 1, forward=2)
+
+        mid_msg(Y1, 1).start()
         partner(Y, 0)
         partner(Y, 1)
-        mid_msg(Y1, 1).start()
         step_g(0, 2)
-        step_dx(0, 2)
         arrive(X, 2, forward=3)
         arrive(X, 3)
+        step_dx(0, 2)
         arrive(Y0, 2, forward=3)
         acc_ref[...] = pair_sum(0)
+        rsend[1] = pair_sum(1).astype(BF16)
+
+        @pl.when(low)
+        def _():
+            rs_copy(1, far_mid, 1).start()
+
         arrive(Y1, 2, forward=3)
-        rsend[1] = pair_sum(1).astype(BF16)
-        rs_copy(1, far_mid, 1).start()
+
+        @pl.when(jnp.logical_not(low))
+        def _():
+            rs_copy(1, far_mid, 1).start()
+
         partner(X, 2)
         partner(X, 3)
         step_u(2, 2)
@@ -291,29 +354,35 @@
         partner(Y, 3)
         step_g(2, 2)
         step_dx(2, 2)
+        first_dw()
         mid_ref[...] = pair_sum(2).astype(BF16)
         last_ref[...] = (pair_sum(3) + rs_recv(1)).astype(BF16)
         acc_ref[...] += rs_recv(0)
         drain(8 + 1)
 
 
-def _dw_kernel(x, dz, zz, y, dw1, dw2, b1, b2, sem):
-    dims = (((0,), (0,)), ((), ()))
+def _dw_kernel(x, dz, zz, y, pre, dw1, dw2, b1, b2, sem):
     n = sem.shape[1]
     hb, fb = x.shape[1] // n, zz.shape[1] // n
 
     def out(j, i):
         src, dst, m = ((b1, dw1, hb), (b2, dw2, fb))[j]
         s = pl.ds(i * m, m)
+        if j == 0 and (i + 1) * hb <= pre.shape[0]:
+            src = pre
         return pltpu.make_async_copy(src.at[s, :], dst.at[s, :], sem.at[j, i])
 
+    done = pre.shape[0] // hb
+    for i in range(done):
+        out(0, i).start()
     for i in range(n):
-        b1[pl.ds(i * hb, hb), :] = lax.dot_general(
-            x[:, pl.ds(i * hb, hb)], dz[...], dims, preferred_element_type=F32)
-        out(0, i).start()
         b2[pl.ds(i * fb, fb), :] = lax.dot_general(
-            zz[:, pl.ds(i * fb, fb)], y[...], dims, preferred_element_type=F32)
+            zz[:, pl.ds(i * fb, fb)], y[...], TN, preferred_element_type=F32)
         out(1, i).start()
+        if i >= done:
+            b1[pl.ds(i * hb, hb), :] = lax.dot_general(
+                x[:, pl.ds(i * hb, hb)], dz[...], TN, preferred_element_type=F32)
+            out(0, i).start()
     for i in range(n):
         out(0, i).wait()
         out(1, i).wait()
@@ -328,18 +397,18 @@
         sem = pltpu.SemaphoreType.DMA
         vspec = pl.BlockSpec(memory_space=vm)
         hbm = pl.BlockSpec(memory_space=pltpu.HBM)
-        xg, yg, zg, dzg, acc, last, mid = pl.pallas_call(
+        xg, yg, zg, dzg, acc, last, mid, pre = pl.pallas_call(
             lambda *refs: _gather_kernel(rows, *refs),
             out_shape=(vm((n, h), BF16), vm((n, h), BF16), vm((n, f), BF16), vm((n, f), BF16),
-                       vm((rows, h), F32), vm((rows, h), BF16), vm((rows, h), BF16)),
+                       vm((rows, h), F32), vm((rows, h), BF16), vm((rows, h), BF16), vm((h // 4, f), F32)),
             in_specs=[hbm] * 4,
-            out_specs=(vspec,) * 7,
+            out_specs=(vspec,) * 8,
             scratch_shapes=[
                 vm((n, f), F32),
                 vm((h, f), BF16), vm((f, h), BF16), vm((f, h), BF16), vm((h, f), BF16),
                 vm((n, h), F32), vm((4, rows, h), BF16), vm((4, rows, h), BF16),
                 vm((3, rows, h), BF16), vm((2, rows, h), BF16),
-                sem((2,)), sem(((f + h) // 256,)), sem(()), sem((3, 4)), sem((3, 4)), sem((5,)), sem((3,)),
+                sem((2,)), sem((6,)), sem(()), sem((8,)), sem((9,)), sem((5,)), sem((3,)), pltpu.SemaphoreType.REGULAR,
             ],
             compiler_params=pltpu.CompilerParams(
                 collective_id=0, has_side_effects=True, vmem_limit_bytes=40 * MIB),
@@ -352,14 +421,14 @@
         dw1, dw2 = pl.pallas_call(
             _dw_kernel,
             out_shape=(jax.ShapeDtypeStruct((h, f), F32), jax.ShapeDtypeStruct((f, h), F32)),
-            in_specs=[vspec] * 4,
+            in_specs=[vspec] * 5,
             out_specs=(hbm,) * 2,
             scratch_shapes=[vm((h, f), F32), vm((f, h), F32), sem((2, steps))],
             compiler_params=pltpu.CompilerParams(vmem_limit_bytes=24 * MIB),
             cost_estimate=pl.CostEstimate(
                 flops=4 * n * h * f, bytes_accessed=8 * h * f, transcendentals=0),
             name='dw',
-        )(xg, dzg, zg, yg)
+        )(xg, dzg, zg, yg, pre)
         dx = (acc + far.astype(F32) + mid.astype(F32)).astype(BF16)
         return dx, dw1, dw2
 

time: 35.6 us -> 37 us (1.039)
  the two profiles are of different devices: /device:TPU:0 before, /device:TPU:9 now
where the time goes in v5:
time: 37 us; the launch traced here: 36.9 us
  Pallas kernels  28 us (76%)
  starting transfers between devices  7 us (19%)
  other arithmetic  0.7 us (2%)
  between operations  0.66 us (2%)
  waiting for transfers between devices  0.51 us (1%)
    pallas_call x1, Pallas kernels, body(): pl.pallas_call(lambda *refs: _gather_kernel(rows, *refs), out_shape=(vm((...  22 us
    pallas_call x1, Pallas kernels, body(): pl.pallas_call(_dw_kernel, out_shape=(jax.ShapeDtypeStruct((h, f), F32),...  5.96 us
    ppermute x1, starting transfers between devices, body(): lax.ppermute(mid, 'tp', [(0, 1), (1, 0), (2, 4), (3, 5), (4, 2), (5, 3),...  4.28 us
    ppermute x1, starting transfers between devices, body(): lax.ppermute(last, 'tp', [(2 * a + c, 2 * b + c) for a, b in hops for c i...  2.72 us
  transfers between devices with their start and end apart: 2, of which 1 were waited for; matrix products, arithmetic and copies ran while one was open for 0% of the time, Pallas kernels for 16%

profile of v5, /device:TPU:9, one launch (start us, length us, event | category | flops | bytes accessed | tf_op | source)
XLA Modules:
  0.0 36.9 jit_solution(5095922161763846428)
XLA Ops:
  0.6 22.0 %gather_dx.1 = (bf16[256,2048]{1,0:T(8,128)(2,1)S(1)}, bf16[256,2048]{1,0:T(8,128)(2,1)S(1)}, bf16[256,1024]{1,0:T(8,128)(2,1)S(1)}, bf16[256,1024]{1,0:T(8,128)...) custom-call(bf16[32,2048]{1,0:T(8,128)(2,1)} %refs_0_.1, ...), custom_call_target="tpu_custom_call" | custom-call | tf_op jit(solution)/shard_map/gather_dx/pallas_call | solution.py:400
  22.7 2.7 %collective-permute-start = (bf16[32,2048]{1,0:T(8,128)(2,1)S(1)}, bf16[32,2048]{1,0:T(8,128)(2,1)S(1)}, u32[]{:S(2)}, u32[]{:S(2)}) collective-permute-start(bf16[32,2048]{1,0:T(8,128)(2,1)S(1)} %get-tuple-element.14), channel_id=1, source_target_pairs={{0,4},{1,5},{4,6},{5,7},{6,2},{7,3},{2,0},{3,1},{8,12},{9,13},{12,... | collective-permute-start | bytes 393224 | tf_op jit(solution)/shard_map/ppermute | solution.py:419
  25.4 4.3 %collective-permute-start.1 = (bf16[32,2048]{1,0:T(8,128)(2,1)S(1)}, bf16[32,2048]{1,0:T(8,128)(2,1)S(1)}, u32[]{:S(2)}, u32[]{:S(2)}) collective-permute-start(bf16[32,2048]{1,0:T(8,128)(2,1)S(1)} %get-tuple-element.15), channel_id=1, source_target_pairs={{0,1},{1,0},{2,4},{3,5},{4,2},{5,3},{6,7},{7,6},{8,9},{9,8},{10,12... | collective-permute-start | bytes 393224 | tf_op jit(solution)/shard_map/ppermute | solution.py:417
  29.7 6.0 %dw.1 = (f32[2048,1024]{1,0:T(8,128)}, f32[1024,2048]{1,0:T(8,128)}) custom-call(bf16[256,2048]{1,0:T(8,128)(2,1)S(1)} %get-tuple-element.16.x, bf16[256,1024]{1,0:T(8,128)(2,1)S(1)} %get-tuple-element.17.dz, bf16[256,1024]{1,0:T(8,128)(2,1)S(1)} %get-tuple-element.18.zz, bf16[256,2048]{1,0:T(8,128)(2,1)S(1)} %get-tuple-element.19.y, ...), custom_call_target="tpu_custom_call" | custom-call | flops 2147483648 | bytes 16777216 | tf_op jit(solution)/shard_map/dw/pallas_call | solution.py:421
  35.6 0.0 collective-permute-done
  35.7 0.5 %collective-permute-done.1 = bf16[32,2048]{1,0:T(8,128)(2,1)S(1)} collective-permute-done((bf16[32,2048]{1,0:T(8,128)(2,1)S(1)}, bf16[32,2048]{1,0:T(8,128)(2,1)S(1)}, u32[]{:S(2)}, u32[]{:S(2)}) %collective-permute-start.1) | collective-permute-done | bytes 131104 | tf_op jit(solution)/shard_map/ppermute | solution.py:417
  36.2 0.7 %add_convert_fusion = bf16[32,2048]{1,0:T(8,128)(2,1)} fusion(bf16[32,2048]{1,0:T(8,128)(2,1)S(1)} %collective-permute-done.1, f32[32,2048]{1,0:T(8,128)S(1)} %get-tuple-element.13, bf16[32,2048]{1,0:T(8,128)(2,1)S(1)} %collective-permute-done), kind=kLoop, calls=%fused_computation | loop fusion | flops 327680 | bytes 655360 | tf_op jit(solution)/shard_map/convert_element_type | solution.py:432
Async XLA Ops:
  22.7 13.0 %collective-permute-start = (bf16[32,2048]{1,0:T(8,128)(2,1)S(1)}, bf16[32,2048]{1,0:T(8,128)(2,1)S(1)}, u32[]{:S(2)}, u32[]{:S(2)}) collective-permute-start(bf16[32,2048]{1,0:T(8,128)(2,1)S(1)} %get-tuple-element.14), channel_id=1, source_target_pairs={{0,4},{1,5},{4,6},{5,7},{6,2},{7,3},{2,0},{3,1},{8,12},{9,13},{12,... | collective-permute-start | bytes 393224 | tf_op jit(solution)/shard_map/ppermute | solution.py:419
  25.4 10.8 %collective-permute-start.1 = (bf16[32,2048]{1,0:T(8,128)(2,1)S(1)}, bf16[32,2048]{1,0:T(8,128)(2,1)S(1)}, u32[]{:S(2)}, u32[]{:S(2)}) collective-permute-start(bf16[32,2048]{1,0:T(8,128)(2,1)S(1)} %get-tuple-element.15), channel_id=1, source_target_pairs={{0,1},{1,0},{2,4},{3,5},{4,2},{5,3},{6,7},{7,6},{8,9},{9,8},{10,12... | collective-permute-start | bytes 393224 | tf_op jit(solution)/shard_map/ppermute | solution.py:417

commit v6 on v5

--- a/solution.py
+++ b/solution.py
@@ -36,6 +36,7 @@
     far_mid, far_end = 3 - near_mid, 3 - near_end
     is_end = z == near_end
     is_mid = jnp.logical_not(is_end)
+    parts = ((0, 512), (512, 512), (1024, 1024))
 
     def dev(chip, core):
         return {'tp': 2 * chip + core}
@@ -47,9 +48,9 @@
         return yg.at[r, pl.ds((a - Y0) * (h // 2), h // 2)]
 
     def flag(a, slot):
-        return {X: slot, Y: 4 + slot, Y0: 4 + slot, Y1: 8}[a]
-
-    loads = [pltpu.make_async_copy(src, block(a, 0, c), in_sem.at[a]) for a, src in ((X, x_hbm), (Y, y_hbm))]
+        return {X: 2 * slot, Y: 2 * slot + 1, Y0: 2 * slot + 1, Y1: 8}[a]
+
+    loads = [pltpu.make_async_copy(src, block(a, 0, c), in_sem) for a, src in ((X, x_hbm), (Y, y_hbm))]
     wloads = []
     for hbm, w, n in ((w2_hbm, w2, 4), (w1_hbm, w1, 2)):
         for i in range(n):
@@ -80,8 +81,8 @@
     def _():
         greet(far_mid, c)
 
-    for cp in loads:
-        cp.wait()
+    both = xg.at[pl.ds(0, chunk), :]
+    pltpu.make_async_copy(both, both, in_sem).wait()
     for cp in wloads:
         cp.start()
 
@@ -96,7 +97,7 @@
     def ag_copy(a, slot, chip, to_slot):
         return pltpu.make_async_remote_copy(
             src_ref=block(a, slot, c), dst_ref=block(a, to_slot, c),
-            send_sem=ag_send, recv_sem=ag_recv.at[flag(a, to_slot) - 1],
+            send_sem=ag_send, recv_sem=ag_recv.at[flag(a, to_slot) - 2],
             device_id=dev(chip, c), device_id_type=MESH)
 
     def share(a, slot):
@@ -113,7 +114,7 @@
 
     def arrive(a, slot, forward=None):
         dst = block(a, slot, c)
-        pltpu.make_async_copy(dst, dst, ag_recv.at[flag(a, slot) - 1]).wait()
+        pltpu.make_async_copy(dst, dst, ag_recv.at[flag(a, slot) - 2]).wait()
         if forward is not None:
             mid_msg(a, forward).start()
         share(a, slot).start()
@@ -123,9 +124,9 @@
 
     def step_u(slot, m=1, half=None):
         r = pl.ds(slot * chunk, m * chunk)
-        nb = f if half is None else f // 2
-
-        @pl.loop(half or 0, (half or 0) + 1)
+        nb = f // 2
+
+        @pl.loop(half or 0, 2 if half is None else half + 1)
         def _(n):
             s = pl.ds(pl.multiple_of(n * nb, nb), nb)
             u = jnp.dot(xg[r, :], w1[:, s], preferred_element_type=F32).astype(BF16)
@@ -157,11 +158,11 @@
 
     def step_dx(slot, m=1, half=None):
         r = pl.ds(slot * chunk, m * chunk)
-        per = h // 1024 if half is None else h // 2048
-
-        @pl.loop(0, per)
+        first, n, nb = (0, h // 1024, 1024) if half is None else (parts[half][0], 1, parts[half][1])
+
+        @pl.loop(0, n)
         def _(n):
-            s = pl.ds(pl.multiple_of(((half or 0) * per + n) * 1024, 1024), 1024)
+            s = pl.ds(pl.multiple_of(first + n * nb, nb if half is None else 128), nb)
             pdx[r, s] = jnp.dot(dzs[r, :], w1t[:, s], preferred_element_type=F32)
             for k in range(slot, slot + m):
                 psend[k, :, s] = part(k, 1 - c, s).astype(BF16)
@@ -177,12 +178,12 @@
         return pdx[pl.ds(pl.multiple_of(k * chunk + core * rows, rows), rows), s]
 
     def cols(half):
-        return slice(None) if half is None else pl.ds(half * (h // 2), h // 2)
+        return slice(None) if half is None else pl.ds(*parts[half])
 
     def pair_copy(k, s, half=None):
         return pltpu.make_async_remote_copy(
             src_ref=psend.at[k, :, s], dst_ref=precv.at[k, :, s], send_sem=ag_send,
-            recv_sem=p_recv.at[4 if half == 1 else k],
+            recv_sem=p_recv.at[3 + half if half else k],
             device_id=dev(z, 1 - c), device_id_type=MESH)
 
     def pair_sum(k, half=None):
@@ -194,13 +195,13 @@
         s = cols(half)
         return pltpu.make_async_remote_copy(
             src_ref=rsend.at[k, :, s], dst_ref=rrecv.at[i, :, s], send_sem=ag_send,
-            recv_sem=r_recv.at[2 if half == 1 else i],
+            recv_sem=r_recv.at[1 + half if half else i],
             device_id=dev(chip, c), device_id_type=MESH)
 
     def rs_recv(i, half=None):
         s = cols(half)
         dst = rrecv.at[i, :, s]
-        pltpu.make_async_copy(dst, dst, r_recv.at[2 if half == 1 else i]).wait()
+        pltpu.make_async_copy(dst, dst, r_recv.at[1 + half if half else i]).wait()
         return rrecv[i, :, s].astype(F32)
 
     def drain(n):
@@ -240,6 +241,59 @@
             wloads[4 + i // 4].wait()
         r = pl.ds(i * (h // 8), h // 8)
         w1t[:, r] = w1[r, :].T
+
+    @pl.when(is_mid)
+    def _():
+        partner(X, 0)
+        step_u(0)
+        arrive(X, 1, forward=2)
+
+        @pl.when(low_mid)
+        def _():
+            pl.semaphore_wait(met, 1)
+
+        mid_msg(X, 1).start()
+
+        @pl.when(low)
+        def _():
+            arrive(Y, 1, forward=2)
+            mid_msg(Y0, 1).start()
+
+        partner(X, 1)
+        step_u(1)
+
+        @pl.when(jnp.logical_not(low))
+        def _():
+            mid_msg(Y0, 1).start()
+            arrive(Y, 1, forward=2)
+
+        mid_msg(Y1, 1).start()
+        partner(Y, 0)
+        partner(Y, 1)
+        step_g(0, 2)
+        arrive(X, 2, forward=3)
+        arrive(X, 3)
+        step_dx(0, 2)
+        arrive(Y0, 2, forward=3)
+        acc_ref[...] = pair_sum(0)
+        rsend[1] = pair_sum(1).astype(BF16)
+
+        rs_copy(1, far_mid, 1).start()
+        arrive(Y1, 2, forward=3)
+        partner(X, 2)
+        partner(X, 3)
+        step_u(2, 2)
+        arrive(Y, 3)
+        partner(Y0, 2)
+        partner(Y1, 2)
+        partner(Y, 3)
+        step_g(2, 2)
+        step_dx(2, 2)
+        first_dw()
+        mid_ref[...] = pair_sum(2).astype(BF16)
+        last_ref[...] = (pair_sum(3) + rs_recv(1)).astype(BF16)
+        acc_ref[...] += rs_recv(0)
+        drain(8 + 1)
 
     @pl.when(is_end)
     def _():
@@ -263,20 +317,21 @@
         rs_copy(1, near_mid, 0).start()
         partner(Y, 2)
         step_g(2)
-        for i in (0, 1):
+        for i in range(len(parts)):
             step_dx(2, half=i)
+        rsend[2, :, cols(0)] = pair_sum(2, 0).astype(BF16)
+        rs_copy(2, far_end, 0, 0).start()
         arrive(X, 3)
-        for i in (0, 1):
+        for i in range(1, len(parts)):
             rsend[2, :, cols(i)] = pair_sum(2, i).astype(BF16)
             rs_copy(2, far_end, 0, i).start()
 
         @pl.when(c == 1)
         def _():
             arrive(Y0, 3)
+            arrive(Y1, 3)
             partner(X, 3)
-            step_u(3, half=0)
-            arrive(Y1, 3)
-            step_u(3, half=1)
+            step_u(3)
             partner(Y0, 3)
             half_g(3, 0)
 
@@ -295,70 +350,9 @@
         first_dw()
         mid_ref[...] = jnp.zeros_like(mid_ref)
         last_ref[...] = pair_sum(3).astype(BF16)
-        for i in (0, 1):
+        for i in range(len(parts)):
             acc_ref[:, cols(i)] += rs_recv(0, i)
         drain(4 + 2)
-
-    @pl.when(is_mid)
-    def _():
-        partner(X, 0)
-        step_u(0)
-        arrive(X, 1, forward=2)
-
-        @pl.when(low_mid)
-        def _():
-            pl.semaphore_wait(met, 1)
-
-        mid_msg(X, 1).start()
-
-        @pl.when(low)
-        def _():
-            arrive(Y, 1, forward=2)
-            mid_msg(Y0, 1).start()
-
-        partner(X, 1)
-        step_u(1)
-
-        @pl.when(jnp.logical_not(low))
-        def _():
-            mid_msg(Y0, 1).start()
-            arrive(Y, 1, forward=2)
-
-        mid_msg(Y1, 1).start()
-        partner(Y, 0)
-        partner(Y, 1)
-        step_g(0, 2)
-        arrive(X, 2, forward=3)
-        arrive(X, 3)
-        step_dx(0, 2)
-        arrive(Y0, 2, forward=3)
-        acc_ref[...] = pair_sum(0)
-        rsend[1] = pair_sum(1).astype(BF16)
-
-        @pl.when(low)
-        def _():
-            rs_copy(1, far_mid, 1).start()
-
-        arrive(Y1, 2, forward=3)
-
-        @pl.when(jnp.logical_not(low))
-        def _():
-            rs_copy(1, far_mid, 1).start()
-
-        partner(X, 2)
-        partner(X, 3)
-        step_u(2, 2)
-        arrive(Y, 3)
-        partner(Y0, 2)
-        partner(Y1, 2)
-        partner(Y, 3)
-        step_g(2, 2)
-        step_dx(2, 2)
-        first_dw()
-        mid_ref[...] = pair_sum(2).astype(BF16)
-        last_ref[...] = (pair_sum(3) + rs_recv(1)).astype(BF16)
-        acc_ref[...] += rs_recv(0)
-        drain(8 + 1)
 
 
 def _dw_kernel(x, dz, zz, y, pre, dw1, dw2, b1, b2, sem):
@@ -408,7 +402,7 @@
                 vm((h, f), BF16), vm((f, h), BF16), vm((f, h), BF16), vm((h, f), BF16),
                 vm((n, h), F32), vm((4, rows, h), BF16), vm((4, rows, h), BF16),
                 vm((3, rows, h), BF16), vm((2, rows, h), BF16),
-                sem((2,)), sem((6,)), sem(()), sem((8,)), sem((9,)), sem((5,)), sem((3,)), pltpu.SemaphoreType.REGULAR,
+                sem(()), sem((6,)), sem(()), sem((7,)), sem((9,)), sem((6,)), sem((4,)), pltpu.SemaphoreType.REGULAR,
             ],
             compiler_params=pltpu.CompilerParams(
                 collective_id=0, has_side_effects=True, vmem_limit_bytes=40 * MIB),

time: 37 us -> 37.4 us (1.011)
  starting transfers between devices: 7 us -> 7.47 us
    ppermute x1, starting transfers between devices: 4.28 us -> 4.69 us  [body(): lax.ppermute(mid, 'tp', [(0, 1), (1, 0), (2, 4), (3, 5), (4, 2), (5, 3),...]
where the time goes in v6:
time: 37.4 us; the launch traced here: 37.3 us
  Pallas kernels  27.9 us (75%)
  starting transfers between devices  7.47 us (20%)
  other arithmetic  0.7 us (2%)
  between operations  0.66 us (2%)
  waiting for transfers between devices  0.52 us (1%)
    pallas_call x1, Pallas kernels, body(): pl.pallas_call(lambda *refs: _gather_kernel(rows, *refs), out_shape=(vm((...  21.9 us
    pallas_call x1, Pallas kernels, body(): pl.pallas_call(_dw_kernel, out_shape=(jax.ShapeDtypeStruct((h, f), F32),...  5.96 us
    ppermute x1, starting transfers between devices, body(): lax.ppermute(mid, 'tp', [(0, 1), (1, 0), (2, 4), (3, 5), (4, 2), (5, 3),...  4.69 us
    ppermute x1, starting transfers between devices, body(): lax.ppermute(last, 'tp', [(2 * a + c, 2 * b + c) for a, b in hops for c i...  2.78 us
  transfers between devices with their start and end apart: 2, of which 1 were waited for; matrix products, arithmetic and copies ran while one was open for 0% of the time, Pallas kernels for 16%

profile of v6, /device:TPU:9, one launch (start us, length us, event | category | flops | bytes accessed | tf_op | source)
XLA Modules:
  0.0 37.3 jit_solution(7126283967800049749)
XLA Ops:
  0.6 21.9 %gather_dx.1 = (bf16[256,2048]{1,0:T(8,128)(2,1)S(1)}, bf16[256,2048]{1,0:T(8,128)(2,1)S(1)}, bf16[256,1024]{1,0:T(8,128)(2,1)S(1)}, bf16[256,1024]{1,0:T(8,128)...) custom-call(bf16[32,2048]{1,0:T(8,128)(2,1)} %refs_0_.1, ...), custom_call_target="tpu_custom_call" | custom-call | tf_op jit(solution)/shard_map/gather_dx/pallas_call | solution.py:394
  22.6 2.8 %collective-permute-start = (bf16[32,2048]{1,0:T(8,128)(2,1)S(1)}, bf16[32,2048]{1,0:T(8,128)(2,1)S(1)}, u32[]{:S(2)}, u32[]{:S(2)}) collective-permute-start(bf16[32,2048]{1,0:T(8,128)(2,1)S(1)} %get-tuple-element.14), channel_id=1, source_target_pairs={{0,4},{1,5},{4,6},{5,7},{6,2},{7,3},{2,0},{3,1},{8,12},{9,13},{12,... | collective-permute-start | bytes 393224 | tf_op jit(solution)/shard_map/ppermute | solution.py:413
  25.4 4.7 %collective-permute-start.1 = (bf16[32,2048]{1,0:T(8,128)(2,1)S(1)}, bf16[32,2048]{1,0:T(8,128)(2,1)S(1)}, u32[]{:S(2)}, u32[]{:S(2)}) collective-permute-start(bf16[32,2048]{1,0:T(8,128)(2,1)S(1)} %get-tuple-element.15), channel_id=1, source_target_pairs={{0,1},{1,0},{2,4},{3,5},{4,2},{5,3},{6,7},{7,6},{8,9},{9,8},{10,12... | collective-permute-start | bytes 393224 | tf_op jit(solution)/shard_map/ppermute | solution.py:411
  30.1 6.0 %dw.1 = (f32[2048,1024]{1,0:T(8,128)}, f32[1024,2048]{1,0:T(8,128)}) custom-call(bf16[256,2048]{1,0:T(8,128)(2,1)S(1)} %get-tuple-element.16.x, bf16[256,1024]{1,0:T(8,128)(2,1)S(1)} %get-tuple-element.17.dz, bf16[256,1024]{1,0:T(8,128)(2,1)S(1)} %get-tuple-element.18.zz, bf16[256,2048]{1,0:T(8,128)(2,1)S(1)} %get-tuple-element.19.y, ...), custom_call_target="tpu_custom_call" | custom-call | flops 2147483648 | bytes 16777216 | tf_op jit(solution)/shard_map/dw/pallas_call | solution.py:415
  36.0 0.0 collective-permute-done
  36.0 0.5 %collective-permute-done.1 = bf16[32,2048]{1,0:T(8,128)(2,1)S(1)} collective-permute-done((bf16[32,2048]{1,0:T(8,128)(2,1)S(1)}, bf16[32,2048]{1,0:T(8,128)(2,1)S(1)}, u32[]{:S(2)}, u32[]{:S(2)}) %collective-permute-start.1) | collective-permute-done | bytes 131104 | tf_op jit(solution)/shard_map/ppermute | solution.py:411
  36.6 0.7 %add_convert_fusion = bf16[32,2048]{1,0:T(8,128)(2,1)} fusion(bf16[32,2048]{1,0:T(8,128)(2,1)S(1)} %collective-permute-done.1, f32[32,2048]{1,0:T(8,128)S(1)} %get-tuple-element.13, bf16[32,2048]{1,0:T(8,128)(2,1)S(1)} %collective-permute-done), kind=kLoop, calls=%fused_computation | loop fusion | flops 327680 | bytes 655360 | tf_op jit(solution)/shard_map/convert_element_type | solution.py:426
Async XLA Ops:
  22.6 13.4 %collective-permute-start = (bf16[32,2048]{1,0:T(8,128)(2,1)S(1)}, bf16[32,2048]{1,0:T(8,128)(2,1)S(1)}, u32[]{:S(2)}, u32[]{:S(2)}) collective-permute-start(bf16[32,2048]{1,0:T(8,128)(2,1)S(1)} %get-tuple-element.14), channel_id=1, source_target_pairs={{0,4},{1,5},{4,6},{5,7},{6,2},{7,3},{2,0},{3,1},{8,12},{9,13},{12,... | collective-permute-start | bytes 393224 | tf_op jit(solution)/shard_map/ppermute | solution.py:413
  25.4 11.2 %collective-permute-start.1 = (bf16[32,2048]{1,0:T(8,128)(2,1)S(1)}, bf16[32,2048]{1,0:T(8,128)(2,1)S(1)}, u32[]{:S(2)}, u32[]{:S(2)}) collective-permute-start(bf16[32,2048]{1,0:T(8,128)(2,1)S(1)} %get-tuple-element.15), channel_id=1, source_target_pairs={{0,1},{1,0},{2,4},{3,5},{4,2},{5,3},{6,7},{7,6},{8,9},{9,8},{10,12... | collective-permute-start | bytes 393224 | tf_op jit(solution)/shard_map/ppermute | solution.py:411

commit v7 on v6

--- a/solution.py
+++ b/solution.py
@@ -356,7 +356,7 @@
 
 
 def _dw_kernel(x, dz, zz, y, pre, dw1, dw2, b1, b2, sem):
-    n = sem.shape[1]
+    n = 8
     hb, fb = x.shape[1] // n, zz.shape[1] // n
 
     def out(j, i):
@@ -364,7 +364,7 @@
         s = pl.ds(i * m, m)
         if j == 0 and (i + 1) * hb <= pre.shape[0]:
             src = pre
-        return pltpu.make_async_copy(src.at[s, :], dst.at[s, :], sem.at[j, i])
+        return pltpu.make_async_copy(src.at[s, :], dst.at[s, :], sem)
 
     done = pre.shape[0] // hb
     for i in range(done):
@@ -377,9 +377,8 @@
             b1[pl.ds(i * hb, hb), :] = lax.dot_general(
                 x[:, pl.ds(i * hb, hb)], dz[...], TN, preferred_element_type=F32)
             out(0, i).start()
-    for i in range(n):
-        out(0, i).wait()
-        out(1, i).wait()
+    pltpu.make_async_copy(b1, dw1, sem).wait()
+    pltpu.make_async_copy(b2, dw2, sem).wait()
 
 
 def solution(mesh):
@@ -411,13 +410,12 @@
         mid = lax.ppermute(mid, 'tp', [(0, 1), (1, 0), (2, 4), (3, 5), (4, 2), (5, 3), (6, 7), (7, 6)])
         hops = ((0, 2), (2, 3), (3, 1), (1, 0))
         far = lax.ppermute(last, 'tp', [(2 * a + c, 2 * b + c) for a, b in hops for c in (0, 1)])
-        steps = 8
         dw1, dw2 = pl.pallas_call(
             _dw_kernel,
             out_shape=(jax.ShapeDtypeStruct((h, f), F32), jax.ShapeDtypeStruct((f, h), F32)),
             in_specs=[vspec] * 5,
             out_specs=(hbm,) * 2,
-            scratch_shapes=[vm((h, f), F32), vm((f, h), F32), sem((2, steps))],
+            scratch_shapes=[vm((h, f), F32), vm((f, h), F32), sem(())],
             compiler_params=pltpu.CompilerParams(vmem_limit_bytes=24 * MIB),
             cost_estimate=pl.CostEstimate(
                 flops=4 * n * h * f, bytes_accessed=8 * h * f, transcendentals=0),

time: 37.4 us -> 37.4 us (level)
  no operation moved by 1% of the time
where the time goes in v7:
time: 37.4 us; the launch traced here: 37.3 us
  Pallas kernels  27.8 us (74%)
  starting transfers between devices  7.47 us (20%)
  other arithmetic  0.7 us (2%)
  waiting for transfers between devices  0.66 us (2%)
  between operations  0.66 us (2%)
    pallas_call x1, Pallas kernels, body(): pl.pallas_call(lambda *refs: _gather_kernel(rows, *refs), out_shape=(vm((...  21.9 us
    pallas_call x1, Pallas kernels, body(): pl.pallas_call(_dw_kernel, out_shape=(jax.ShapeDtypeStruct((h, f), F32),...  5.82 us
    ppermute x1, starting transfers between devices, body(): lax.ppermute(mid, 'tp', [(0, 1), (1, 0), (2, 4), (3, 5), (4, 2), (5, 3),...  4.69 us
    ppermute x1, starting transfers between devices, body(): lax.ppermute(last, 'tp', [(2 * a + c, 2 * b + c) for a, b in hops for c i...  2.78 us
  transfers between devices with their start and end apart: 2, of which 1 were waited for; matrix products, arithmetic and copies ran while one was open for 0% of the time, Pallas kernels for 16%

profile of v7, /device:TPU:9, one launch (start us, length us, event | category | flops | bytes accessed | tf_op | source)
XLA Modules:
  0.0 37.3 jit_solution(5260654543306312166)
XLA Ops:
  0.6 21.9 %gather_dx.1 = (bf16[256,2048]{1,0:T(8,128)(2,1)S(1)}, bf16[256,2048]{1,0:T(8,128)(2,1)S(1)}, bf16[256,1024]{1,0:T(8,128)(2,1)S(1)}, bf16[256,1024]{1,0:T(8,128)...) custom-call(bf16[32,2048]{1,0:T(8,128)(2,1)} %refs_0_.1, ...), custom_call_target="tpu_custom_call" | custom-call | tf_op jit(solution)/shard_map/gather_dx/pallas_call | solution.py:393
  22.6 2.8 %collective-permute-start = (bf16[32,2048]{1,0:T(8,128)(2,1)S(1)}, bf16[32,2048]{1,0:T(8,128)(2,1)S(1)}, u32[]{:S(2)}, u32[]{:S(2)}) collective-permute-start(bf16[32,2048]{1,0:T(8,128)(2,1)S(1)} %get-tuple-element.14), channel_id=1, source_target_pairs={{0,4},{1,5},{4,6},{5,7},{6,2},{7,3},{2,0},{3,1},{8,12},{9,13},{12,... | collective-permute-start | bytes 393224 | tf_op jit(solution)/shard_map/ppermute | solution.py:412
  25.4 4.7 %collective-permute-start.1 = (bf16[32,2048]{1,0:T(8,128)(2,1)S(1)}, bf16[32,2048]{1,0:T(8,128)(2,1)S(1)}, u32[]{:S(2)}, u32[]{:S(2)}) collective-permute-start(bf16[32,2048]{1,0:T(8,128)(2,1)S(1)} %get-tuple-element.15), channel_id=1, source_target_pairs={{0,1},{1,0},{2,4},{3,5},{4,2},{5,3},{6,7},{7,6},{8,9},{9,8},{10,12... | collective-permute-start | bytes 393224 | tf_op jit(solution)/shard_map/ppermute | solution.py:410
  30.1 5.8 %dw.1 = (f32[2048,1024]{1,0:T(8,128)}, f32[1024,2048]{1,0:T(8,128)}) custom-call(bf16[256,2048]{1,0:T(8,128)(2,1)S(1)} %get-tuple-element.16.x, bf16[256,1024]{1,0:T(8,128)(2,1)S(1)} %get-tuple-element.17.dz, bf16[256,1024]{1,0:T(8,128)(2,1)S(1)} %get-tuple-element.18.zz, bf16[256,2048]{1,0:T(8,128)(2,1)S(1)} %get-tuple-element.19.y, ...), custom_call_target="tpu_custom_call" | custom-call | flops 2147483648 | bytes 16777216 | tf_op jit(solution)/shard_map/dw/pallas_call | solution.py:413
  35.9 0.0 collective-permute-done
  35.9 0.7 %collective-permute-done.1 = bf16[32,2048]{1,0:T(8,128)(2,1)S(1)} collective-permute-done((bf16[32,2048]{1,0:T(8,128)(2,1)S(1)}, bf16[32,2048]{1,0:T(8,128)(2,1)S(1)}, u32[]{:S(2)}, u32[]{:S(2)}) %collective-permute-start.1) | collective-permute-done | bytes 131104 | tf_op jit(solution)/shard_map/ppermute | solution.py:410
  36.6 0.7 %add_convert_fusion = bf16[32,2048]{1,0:T(8,128)(2,1)} fusion(bf16[32,2048]{1,0:T(8,128)(2,1)S(1)} %collective-permute-done.1, f32[32,2048]{1,0:T(8,128)S(1)} %get-tuple-element.13, bf16[32,2048]{1,0:T(8,128)(2,1)S(1)} %collective-permute-done), kind=kLoop, calls=%fused_computation | loop fusion | flops 327680 | bytes 655360 | tf_op jit(solution)/shard_map/convert_element_type | solution.py:424
Async XLA Ops:
  22.6 13.3 %collective-permute-start = (bf16[32,2048]{1,0:T(8,128)(2,1)S(1)}, bf16[32,2048]{1,0:T(8,128)(2,1)S(1)}, u32[]{:S(2)}, u32[]{:S(2)}) collective-permute-start(bf16[32,2048]{1,0:T(8,128)(2,1)S(1)} %get-tuple-element.14), channel_id=1, source_target_pairs={{0,4},{1,5},{4,6},{5,7},{6,2},{7,3},{2,0},{3,1},{8,12},{9,13},{12,... | collective-permute-start | bytes 393224 | tf_op jit(solution)/shard_map/ppermute | solution.py:412
  25.4 11.2 %collective-permute-start.1 = (bf16[32,2048]{1,0:T(8,128)(2,1)S(1)}, bf16[32,2048]{1,0:T(8,128)(2,1)S(1)}, u32[]{:S(2)}, u32[]{:S(2)}) collective-permute-start(bf16[32,2048]{1,0:T(8,128)(2,1)S(1)} %get-tuple-element.15), channel_id=1, source_target_pairs={{0,1},{1,0},{2,4},{3,5},{4,2},{5,3},{6,7},{7,6},{8,9},{9,8},{10,12... | collective-permute-start | bytes 393224 | tf_op jit(solution)/shard_map/ppermute | solution.py:410

commit v8 on v7

--- a/solution.py
+++ b/solution.py
@@ -165,7 +165,7 @@
             s = pl.ds(pl.multiple_of(first + n * nb, nb if half is None else 128), nb)
             pdx[r, s] = jnp.dot(dzs[r, :], w1t[:, s], preferred_element_type=F32)
             for k in range(slot, slot + m):
-                psend[k, :, s] = part(k, 1 - c, s).astype(BF16)
+                psend[k, :, s] = part(k, 1 - mine(half), s).astype(BF16)
                 pair_copy(k, s, half).start()
 
     def first_dw():
@@ -177,6 +177,9 @@
     def part(k, core, s=slice(None)):
         return pdx[pl.ds(pl.multiple_of(k * chunk + core * rows, rows), rows), s]
 
+    def mine(half):
+        return c if half is None else 1 - c
+
     def cols(half):
         return slice(None) if half is None else pl.ds(*parts[half])
 
@@ -189,14 +192,14 @@
     def pair_sum(k, half=None):
         s = cols(half)
         pair_copy(k, s, half).wait_recv()
-        return part(k, c, s) + precv[k, :, s].astype(F32)
+        return part(k, mine(half), s) + precv[k, :, s].astype(F32)
 
     def rs_copy(k, chip, i, half=None):
         s = cols(half)
         return pltpu.make_async_remote_copy(
             src_ref=rsend.at[k, :, s], dst_ref=rrecv.at[i, :, s], send_sem=ag_send,
             recv_sem=r_recv.at[1 + half if half else i],
-            device_id=dev(chip, c), device_id_type=MESH)
+            device_id=dev(chip, mine(half)), device_id_type=MESH)
 
     def rs_recv(i, half=None):
         s = cols(half)
@@ -338,11 +341,12 @@
         @pl.when(c == 0)
         def _():
             partner(X, 3)
-            step_u(3)
+            step_u(3, half=0)
             arrive(Y0, 3)
+            step_u(3, half=1)
+            arrive(Y1, 3)
             partner(Y0, 3)
             half_g(3, 0)
-            arrive(Y1, 3)
 
         partner(Y1, 3)
         half_g(3, 1)

time: 37.4 us -> 37.4 us (level)
  no operation moved by 1% of the time
where the time goes in v8:
time: 37.4 us; the launch traced here: 37.3 us
  Pallas kernels  27.8 us (74%)
  starting transfers between devices  7.47 us (20%)
  other arithmetic  0.7 us (2%)
  waiting for transfers between devices  0.66 us (2%)
  between operations  0.66 us (2%)
    pallas_call x1, Pallas kernels, body(): pl.pallas_call(lambda *refs: _gather_kernel(rows, *refs), out_shape=(vm((...  21.9 us
    pallas_call x1, Pallas kernels, body(): pl.pallas_call(_dw_kernel, out_shape=(jax.ShapeDtypeStruct((h, f), F32),...  5.82 us
    ppermute x1, starting transfers between devices, body(): lax.ppermute(mid, 'tp', [(0, 1), (1, 0), (2, 4), (3, 5), (4, 2), (5, 3),...  4.55 us
    ppermute x1, starting transfers between devices, body(): lax.ppermute(last, 'tp', [(2 * a + c, 2 * b + c) for a, b in hops for c i...  2.92 us
  transfers between devices with their start and end apart: 2, of which 1 were waited for; matrix products, arithmetic and copies ran while one was open for 0% of the time, Pallas kernels for 16%

profile of v8, /device:TPU:9, one launch (start us, length us, event | category | flops | bytes accessed | tf_op | source)
XLA Modules:
  0.0 37.3 jit_solution(10276289168137409832)
XLA Ops:
  0.6 21.9 %gather_dx.1 = (bf16[256,2048]{1,0:T(8,128)(2,1)S(1)}, bf16[256,2048]{1,0:T(8,128)(2,1)S(1)}, bf16[256,1024]{1,0:T(8,128)(2,1)S(1)}, bf16[256,1024]{1,0:T(8,128)...) custom-call(bf16[32,2048]{1,0:T(8,128)(2,1)} %refs_0_.1, ...), custom_call_target="tpu_custom_call" | custom-call | tf_op jit(solution)/shard_map/gather_dx/pallas_call | solution.py:397
  22.6 2.9 %collective-permute-start = (bf16[32,2048]{1,0:T(8,128)(2,1)S(1)}, bf16[32,2048]{1,0:T(8,128)(2,1)S(1)}, u32[]{:S(2)}, u32[]{:S(2)}) collective-permute-start(bf16[32,2048]{1,0:T(8,128)(2,1)S(1)} %get-tuple-element.14), channel_id=1, source_target_pairs={{0,4},{1,5},{4,6},{5,7},{6,2},{7,3},{2,0},{3,1},{8,12},{9,13},{12,... | collective-permute-start | bytes 393224 | tf_op jit(solution)/shard_map/ppermute | solution.py:416
  25.5 4.5 %collective-permute-start.1 = (bf16[32,2048]{1,0:T(8,128)(2,1)S(1)}, bf16[32,2048]{1,0:T(8,128)(2,1)S(1)}, u32[]{:S(2)}, u32[]{:S(2)}) collective-permute-start(bf16[32,2048]{1,0:T(8,128)(2,1)S(1)} %get-tuple-element.15), channel_id=1, source_target_pairs={{0,1},{1,0},{2,4},{3,5},{4,2},{5,3},{6,7},{7,6},{8,9},{9,8},{10,12... | collective-permute-start | bytes 393224 | tf_op jit(solution)/shard_map/ppermute | solution.py:414
  30.1 5.8 %dw.1 = (f32[2048,1024]{1,0:T(8,128)}, f32[1024,2048]{1,0:T(8,128)}) custom-call(bf16[256,2048]{1,0:T(8,128)(2,1)S(1)} %get-tuple-element.16.x, bf16[256,1024]{1,0:T(8,128)(2,1)S(1)} %get-tuple-element.17.dz, bf16[256,1024]{1,0:T(8,128)(2,1)S(1)} %get-tuple-element.18.zz, bf16[256,2048]{1,0:T(8,128)(2,1)S(1)} %get-tuple-element.19.y, ...), custom_call_target="tpu_custom_call" | custom-call | flops 2147483648 | bytes 16777216 | tf_op jit(solution)/shard_map/dw/pallas_call | solution.py:417
  35.9 0.0 collective-permute-done
  35.9 0.7 %collective-permute-done.1 = bf16[32,2048]{1,0:T(8,128)(2,1)S(1)} collective-permute-done((bf16[32,2048]{1,0:T(8,128)(2,1)S(1)}, bf16[32,2048]{1,0:T(8,128)(2,1)S(1)}, u32[]{:S(2)}, u32[]{:S(2)}) %collective-permute-start.1) | collective-permute-done | bytes 131104 | tf_op jit(solution)/shard_map/ppermute | solution.py:414
  36.6 0.7 %add_convert_fusion = bf16[32,2048]{1,0:T(8,128)(2,1)} fusion(bf16[32,2048]{1,0:T(8,128)(2,1)S(1)} %collective-permute-done.1, f32[32,2048]{1,0:T(8,128)S(1)} %get-tuple-element.13, bf16[32,2048]{1,0:T(8,128)(2,1)S(1)} %collective-permute-done), kind=kLoop, calls=%fused_computation | loop fusion | flops 327680 | bytes 655360 | tf_op jit(solution)/shard_map/convert_element_type | solution.py:428
Async XLA Ops:
  22.6 13.3 %collective-permute-start = (bf16[32,2048]{1,0:T(8,128)(2,1)S(1)}, bf16[32,2048]{1,0:T(8,128)(2,1)S(1)}, u32[]{:S(2)}, u32[]{:S(2)}) collective-permute-start(bf16[32,2048]{1,0:T(8,128)(2,1)S(1)} %get-tuple-element.14), channel_id=1, source_target_pairs={{0,4},{1,5},{4,6},{5,7},{6,2},{7,3},{2,0},{3,1},{8,12},{9,13},{12,... | collective-permute-start | bytes 393224 | tf_op jit(solution)/shard_map/ppermute | solution.py:416
  25.5 11.0 %collective-permute-start.1 = (bf16[32,2048]{1,0:T(8,128)(2,1)S(1)}, bf16[32,2048]{1,0:T(8,128)(2,1)S(1)}, u32[]{:S(2)}, u32[]{:S(2)}) collective-permute-start(bf16[32,2048]{1,0:T(8,128)(2,1)S(1)} %get-tuple-element.15), channel_id=1, source_target_pairs={{0,1},{1,0},{2,4},{3,5},{4,2},{5,3},{6,7},{7,6},{8,9},{9,8},{10,12... | collective-permute-start | bytes 393224 | tf_op jit(solution)/shard_map/ppermute | solution.py:414

commit v9 on v8

--- a/solution.py
+++ b/solution.py
@@ -383,6 +383,15 @@
             out(0, i).start()
     pltpu.make_async_copy(b1, dw1, sem).wait()
     pltpu.make_async_copy(b2, dw2, sem).wait()
+
+
+def _add_kernel(acc, far, mid, dx, buf, sem):
+    half = acc.shape[0] // 2
+    for i in range(2):
+        r = pl.ds(i * half, half)
+        buf[r, :] = (acc[r, :] + far[r, :].astype(F32) + mid[r, :].astype(F32)).astype(BF16)
+        pltpu.make_async_copy(buf.at[r, :], dx.at[r, :], sem).start()
+    pltpu.make_async_copy(buf, dx, sem).wait()
 
 
 def solution(mesh):
@@ -425,7 +434,15 @@
                 flops=4 * n * h * f, bytes_accessed=8 * h * f, transcendentals=0),
             name='dw',
         )(xg, dzg, zg, yg, pre)
-        dx = (acc + far.astype(F32) + mid.astype(F32)).astype(BF16)
+        dx = pl.pallas_call(
+            _add_kernel,
+            out_shape=jax.ShapeDtypeStruct((rows, h), BF16),
+            in_specs=[vspec] * 3,
+            out_specs=hbm,
+            scratch_shapes=[vm((rows, h), BF16), sem(())],
+            compiler_params=pltpu.CompilerParams(vmem_limit_bytes=2 * MIB),
+            name='add',
+        )(acc, far, mid)
         return dx, dw1, dw2
 
     return jax.shard_map(

time: 37.4 us -> 37.4 us (level)
  other arithmetic: 0.7 us -> 0 us
  Pallas kernels: 27.8 us -> 28.4 us
    convert_element_type x1 -> x0, other arithmetic: 0.7 us -> none  [body(): dx = (acc + far.astype(F32) + mid.astype(F32)).astype(BF16)]
    pallas_call x0 -> x1, Pallas kernels: none -> 0.68 us  [body(): pl.pallas_call(_add_kernel, out_shape=jax.ShapeDtypeStruct((rows, h), BF1...]
where the time goes in v9:
time: 37.4 us; the launch traced here: 37.2 us
  Pallas kernels  28.4 us (76%)
  starting transfers between devices  7.47 us (20%)
  waiting for transfers between devices  0.66 us (2%)
  between operations  0.66 us (2%)
    pallas_call x1, Pallas kernels, body(): pl.pallas_call(lambda *refs: _gather_kernel(rows, *refs), out_shape=(vm((...  21.9 us
    pallas_call x1, Pallas kernels, body(): pl.pallas_call(_dw_kernel, out_shape=(jax.ShapeDtypeStruct((h, f), F32),...  5.82 us
    ppermute x1, starting transfers between devices, body(): lax.ppermute(mid, 'tp', [(0, 1), (1, 0), (2, 4), (3, 5), (4, 2), (5, 3),...  4.55 us
    ppermute x1, starting transfers between devices, body(): lax.ppermute(last, 'tp', [(2 * a + c, 2 * b + c) for a, b in hops for c i...  2.92 us
  transfers between devices with their start and end apart: 2, of which 1 were waited for; matrix products, arithmetic and copies ran while one was open for 0% of the time, Pallas kernels for 16%

profile of v9, /device:TPU:9, one launch (start us, length us, event | category | flops | bytes accessed | tf_op | source)
XLA Modules:
  0.0 37.2 jit_solution(6818270996474789081)
XLA Ops:
  0.6 21.9 %gather_dx.1 = (bf16[256,2048]{1,0:T(8,128)(2,1)S(1)}, bf16[256,2048]{1,0:T(8,128)(2,1)S(1)}, bf16[256,1024]{1,0:T(8,128)(2,1)S(1)}, bf16[256,1024]{1,0:T(8,128)...) custom-call(bf16[32,2048]{1,0:T(8,128)(2,1)} %refs_0_.1, ...), custom_call_target="tpu_custom_call" | custom-call | tf_op jit(solution)/shard_map/gather_dx/pallas_call | solution.py:406
  22.6 2.9 %collective-permute-start = (bf16[32,2048]{1,0:T(8,128)(2,1)S(1)}, bf16[32,2048]{1,0:T(8,128)(2,1)S(1)}, u32[]{:S(2)}, u32[]{:S(2)}) collective-permute-start(bf16[32,2048]{1,0:T(8,128)(2,1)S(1)} %get-tuple-element.14), channel_id=1, source_target_pairs={{0,4},{1,5},{4,6},{5,7},{6,2},{7,3},{2,0},{3,1},{8,12},{9,13},{12,... | collective-permute-start | bytes 393224 | tf_op jit(solution)/shard_map/ppermute | solution.py:425
  25.5 4.5 %collective-permute-start.1 = (bf16[32,2048]{1,0:T(8,128)(2,1)S(1)}, bf16[32,2048]{1,0:T(8,128)(2,1)S(1)}, u32[]{:S(2)}, u32[]{:S(2)}) collective-permute-start(bf16[32,2048]{1,0:T(8,128)(2,1)S(1)} %get-tuple-element.15), channel_id=1, source_target_pairs={{0,1},{1,0},{2,4},{3,5},{4,2},{5,3},{6,7},{7,6},{8,9},{9,8},{10,12... | collective-permute-start | bytes 393224 | tf_op jit(solution)/shard_map/ppermute | solution.py:423
  30.1 5.8 %dw.1 = (f32[2048,1024]{1,0:T(8,128)}, f32[1024,2048]{1,0:T(8,128)}) custom-call(bf16[256,2048]{1,0:T(8,128)(2,1)S(1)} %get-tuple-element.16.x, bf16[256,1024]{1,0:T(8,128)(2,1)S(1)} %get-tuple-element.17.dz, bf16[256,1024]{1,0:T(8,128)(2,1)S(1)} %get-tuple-element.18.zz, bf16[256,2048]{1,0:T(8,128)(2,1)S(1)} %get-tuple-element.19.y, ...), custom_call_target="tpu_custom_call" | custom-call | flops 2147483648 | bytes 16777216 | tf_op jit(solution)/shard_map/dw/pallas_call | solution.py:426
  35.9 0.0 collective-permute-done.far
  35.9 0.7 %collective-permute-done.1.mid = bf16[32,2048]{1,0:T(8,128)(2,1)S(1)} collective-permute-done((bf16[32,2048]{1,0:T(8,128)(2,1)S(1)}, bf16[32,2048]{1,0:T(8,128)(2,1)S(1)}, u32[]{:S(2)}, u32[]{:S(2)}) %collective-permute-start.1) | collective-permute-done | bytes 131104 | tf_op jit(solution)/shard_map/ppermute | solution.py:423
  36.6 0.7 %add.1 = bf16[32,2048]{1,0:T(8,128)(2,1)} custom-call(f32[32,2048]{1,0:T(8,128)S(1)} %get-tuple-element.13.acc, bf16[32,2048]{1,0:T(8,128)(2,1)S(1)} %collective-permute-done.far, bf16[32,2048]{1,0:T(8,128)(2,1)S(1)} %collective-permute-done.1.mid), custom_call_target="tpu_custom_call" | custom-call | tf_op jit(solution)/shard_map/add/pallas_call | solution.py:437
Async XLA Ops:
  22.6 13.3 %collective-permute-start = (bf16[32,2048]{1,0:T(8,128)(2,1)S(1)}, bf16[32,2048]{1,0:T(8,128)(2,1)S(1)}, u32[]{:S(2)}, u32[]{:S(2)}) collective-permute-start(bf16[32,2048]{1,0:T(8,128)(2,1)S(1)} %get-tuple-element.14), channel_id=1, source_target_pairs={{0,4},{1,5},{4,6},{5,7},{6,2},{7,3},{2,0},{3,1},{8,12},{9,13},{12,... | collective-permute-start | bytes 393224 | tf_op jit(solution)/shard_map/ppermute | solution.py:425
  25.5 11.0 %collective-permute-start.1 = (bf16[32,2048]{1,0:T(8,128)(2,1)S(1)}, bf16[32,2048]{1,0:T(8,128)(2,1)S(1)}, u32[]{:S(2)}, u32[]{:S(2)}) collective-permute-start(bf16[32,2048]{1,0:T(8,128)(2,1)S(1)} %get-tuple-element.15), channel_id=1, source_target_pairs={{0,1},{1,0},{2,4},{3,5},{4,2},{5,3},{6,7},{7,6},{8,9},{9,8},{10,12... | collective-permute-start | bytes 393224 | tf_op jit(solution)/shard_map/ppermute | solution.py:423
